TPU v7x, 256 devices: a whole 4x4x8 slice. The times are simulated.
256 devices in a mesh: wav: 32 (over y, x, core), lev: 8 (over z).
Axes of the slice: x: 4, y: 4, z: 8, core: 2. Of those that a mesh axis runs over, the one named last changes fastest.
Arguments:
- spectral: bfloat16 [224, 401, 1024], P('wav', None, 'lev'), may hold values from -0.1796875 to 0.1796875
- legendre: bfloat16 [224, 401, 256], P('wav', None, 'lev'), may hold values from -0.4375 to 0.4375
- wave_pair: int32 [224], replicated, may hold values from -1 to 199, as said below
- lat_slot: int32 [256], replicated, may hold values from 0 to 799, as said below
Outputs:
- gridded: bfloat16 [256, 512, 1616], P('wav', 'lev')
Inputs may be any that keep to these rules, and one draw needn't show every extreme that they name: `wave_pair`: each pair number 0 to 199 appears exactly once; all other entries are -1. `lat_slot`: the entries are distinct latitudes.
All inputs are finite; a program needn't handle non-finite values.
Results may differ from a plain program's by a relative error of at most 0.0055.
Values may be sent and summed in bfloat16 or wider, within the bound.
A program may use at most 64 MiB of HBM per device.

v0:
```python
import math

import jax
import jax.numpy as jnp
from jax import lax
from jax.sharding import PartitionSpec as P

NLAT = 800


def from_everyone(shard, axis):
    copies = jnp.broadcast_to(shard, (lax.axis_size(axis), *shard.shape))
    return lax.all_to_all(copies, axis, split_axis=0, concat_axis=0, tiled=True)


def laid_out(blocks, dim):
    dims = list(blocks.shape[1:])
    dims[dim] *= blocks.shape[0]
    return jnp.moveaxis(blocks, 0, dim).reshape(dims)


def gather_directly(shard, axis, dim):
    blocks = from_everyone(shard, axis)
    return laid_out(blocks, dim)


def fold_masks(pair_ids, fold_count, wave_count):
    fold_rows = jnp.arange(fold_count, dtype=jnp.int32)
    filled = pair_ids >= 0
    border = wave_count - pair_ids
    lower = filled[:, None] & (fold_rows[None, :] < border[:, None])
    upper = filled[:, None] & (fold_rows[None, :] >= border[:, None])
    return jnp.stack([lower, upper], axis=1)


def trig_parts(wave_numbers, steps, counts_b):
    residue = wave_numbers[None, None] * steps[None, :, None, None] % counts_b
    angles = residue.astype(jnp.float32) * (2.0 * math.pi) / counts_b.astype(jnp.float32)
    return (jnp.cos(angles), jnp.sin(angles))


def synthesis_table(pair_ids, row_lats, lat_count, lon_width, wave_count):
    filled = pair_ids >= 0
    wave_numbers = jnp.stack([pair_ids, wave_count - 1 - pair_ids], axis=1)
    lon_count = 20 + 4 * jnp.minimum(row_lats, lat_count - 1 - row_lats)
    highest = jnp.minimum(wave_count - 1, (lon_count - 1) // 2)
    counts_b = lon_count[:, None, None, None]
    coarse_count = (lon_width + 63) // 64
    coarse_steps = jnp.arange(coarse_count, dtype=jnp.int32) * 64
    fine_steps = jnp.arange(64, dtype=jnp.int32)
    cos_coarse, sin_coarse = trig_parts(wave_numbers, coarse_steps, counts_b)
    cos_fine, sin_fine = trig_parts(wave_numbers, fine_steps, counts_b)
    cos_all = (
        cos_coarse[:, :, None] * cos_fine[:, None] - sin_coarse[:, :, None] * sin_fine[:, None]
    )
    sin_all = (
        sin_coarse[:, :, None] * cos_fine[:, None] + cos_coarse[:, :, None] * sin_fine[:, None]
    )
    row_total = row_lats.shape[0]
    cos_all = cos_all.reshape(row_total, coarse_count * 64, wave_numbers.shape[0], 2)[:, :lon_width]
    sin_all = sin_all.reshape(row_total, coarse_count * 64, wave_numbers.shape[0], 2)[:, :lon_width]
    columns = jnp.arange(lon_width, dtype=jnp.int32)
    valid = (
        filled[None, None, :, None]
        & (wave_numbers[None, None] <= highest[:, None, None, None])
        & (columns[None, :, None, None] < counts_b)
    )
    factor = jnp.where(wave_numbers == 0, 1.0, 2.0).astype(jnp.float32)[None, None]
    real_part = jnp.where(valid, factor * cos_all, 0.0)
    imag_part = jnp.where(valid, -factor * sin_all, 0.0)
    return jnp.stack([real_part, imag_part], axis=-1).astype(jnp.bfloat16)


def legendre_sum(coefficients, weights, half_masks):
    paired = coefficients.reshape(
        coefficients.shape[0], coefficients.shape[1], coefficients.shape[2] // 2, 2
    )
    masked = jnp.where(
        half_masks[:, :, :, None, None], paired[:, None], jnp.zeros((), paired.dtype)
    )
    summed = jnp.einsum("shtlc,sta->ashcl", masked, weights, preferred_element_type=jnp.float32)
    return summed.astype(jnp.bfloat16)


def on_device(spectral, legendre, wave_pair, lat_slot):
    slot_count = spectral.shape[0]
    fold_count = spectral.shape[1]
    wave_count = fold_count - 1
    lat_count = NLAT
    lon_width = 2 * lat_count + 16
    wav_devices = lax.axis_size("wav")
    wav_index = lax.axis_index("wav")
    own_pairs = lax.dynamic_slice_in_dim(wave_pair, wav_index * slot_count, slot_count)
    half_masks = fold_masks(own_pairs, fold_count, wave_count)
    fourier = legendre_sum(spectral, gather_directly(legendre, "lev", 2), half_masks)
    row_count = lat_slot.shape[0] // wav_devices
    row_lats = lax.dynamic_slice_in_dim(lat_slot, wav_index * row_count, row_count)
    group_rows = max(1, row_count // 25)
    while row_count % group_rows:
        group_rows -= 1
    group_count = row_count // group_rows
    received = lax.all_to_all(fourier, "wav", split_axis=0, concat_axis=1, tiled=True)
    layer_items = received.shape[4]
    grouped = received.reshape((group_count, group_rows) + received.shape[1:])
    lat_groups = row_lats.reshape(group_count, group_rows)

    def one_group(args):
        values, group_lats = args
        basis = synthesis_table(wave_pair, group_lats, lat_count, lon_width, wave_count)
        result = jnp.einsum("rjghc,rghcl->rlj", basis, values, preferred_element_type=jnp.float32)
        return result.astype(jnp.bfloat16)

    gridded_groups = lax.map(one_group, (grouped, lat_groups))
    return gridded_groups.reshape(row_count, layer_items, lon_width)


def solution(mesh):
    return jax.shard_map(
        on_device,
        mesh=mesh,
        in_specs=(P("wav", None, "lev"), P("wav", None, "lev"), P(), P()),
        out_specs=P("wav", "lev", None),
        check_vma=False,
    )
```

profile of v0, /device:TPU:1, one launch (start us, length us, event | category | flops | bytes accessed | tf_op | source)
XLA Modules:
  0.0 264.1 jit_solution(804061478563402776)
XLA Ops:
  0.0 2.4 broadcast_in_dim.98
  2.4 9.1 %all-to-all-start = ((bf16[8,7,401,32]{2,3,1,0:T(8,128)(2,1)}), bf16[8,7,401,32]{2,3,1,0:T(8,128)(2,1)S(1)}, u32[]{:S(2)}, u32[]{:S(2)}) async-start(bf16[8,7,401,32]{2,3,1,0:T(8,128)(2,1)} %broadcast_in_dim.98), calls=%async_computation | async-start | bytes 3670016 | tf_op jit(solution)/shard_map/all_to_all | solution.py:13
  13.0 2.5 broadcast_in_dim.95
  16.9 40.7 %all-to-all-done = bf16[8,7,401,32]{2,3,1,0:T(8,128)(2,1)S(1)} async-done(((bf16[8,7,401,32]{2,3,1,0:T(8,128)(2,1)}), bf16[8,7,401,32]{2,3,1,0:T(8,128)(2,1)S(1)}, u32[]{:S(2)}, u32[]{:S(2)}) %all-to-all-start) | async-done | bytes 1437216 | tf_op jit(solution)/shard_map/all_to_all | solution.py:13
  59.5 1.8 copy.22
  61.3 1.9 reshape.588
  63.2 7.6 %all-to-all-start.1 = ((bf16[32,2,7168]{2,1,0:T(2,128)(2,1)}), bf16[32,2,7168]{2,1,0:T(2,128)(2,1)S(1)}, u32[]{:S(2)}, u32[]{:S(2)}) async-start(bf16[32,2,7168]{2,1,0:T(2,128)(2,1)} %reshape.588), calls=%async_computation.1 | async-start | bytes 1835008 | tf_op jit(solution)/shard_map/all_to_all | solution.py:102
  70.9 15.5 %all-to-all-done.1 = bf16[32,2,7168]{2,1,0:T(2,128)(2,1)S(1)} async-done(((bf16[32,2,7168]{2,1,0:T(2,128)(2,1)}), bf16[32,2,7168]{2,1,0:T(2,128)(2,1)S(1)}, u32[]{:S(2)}, u32[]{:S(2)}) %all-to-all-start.1) | async-done | bytes 917536 | tf_op jit(solution)/shard_map/all_to_all | solution.py:102
  88.2 2.5 copy.25
  90.8 173.3 %while.15 = (s32[]{:T(128)}, bf16[8,1,64,1616]{3,2,1,0:T(8,128)(2,1)}, bf16[8,1,224,2,2,64]{2,5,3,4,1,0:T(8,128)(2,1)}, s32[224]{0:T(256)S(1)}, s32[8,1]{0,1:T(1...) while((s32[]{:T(128)}, ...), condition=%wide.region_1.2_spmd, body=%wide.region_0.1_spmd.sunk | while | flops 196876992 | bytes 53313796 | solution.py:113
  92.6 1.8 fusion.64
  96.2 1.9 slice.24
  98.1 3.6 %copy.36 = f32[1,1616,224,2]{1,2,3,0:T(8,128)} copy(f32[1,1616,224,2]{2,1,3,0:T(8,128)} %slice.24) | data formatting | bytes 5791744 | tf_op jit(solution)/shard_map/while
  101.7 1.9 slice.25
  103.6 3.8 %copy.37 = f32[1,1616,224,2]{1,2,3,0:T(8,128)} copy(f32[1,1616,224,2]{2,1,3,0:T(8,128)} %slice.25) | data formatting | bytes 5791744 | tf_op jit(solution)/shard_map/while
  107.5 2.7 %fusion.66 = (bf16[1616,224,2,1]{0,1,2,3:T(8,128)(2,1)S(1)}, bf16[1616,224,2,1]{0,1,2,3:T(8,128)(2,1)S(1)}) fusion(f32[1,1616,224,2]{1,2,3,0:T(8,128)S(1)} %copy-done.1, f32[224,2]{0,1:T(2,128)S(1)} %get-tuple-element.206, pred[1616]{0:T(1024)(128)(4,1)S(1)} %iota_compare_fusion.2, pred[224,2]{0,1:T(4,128)(4,1)S(1)} %compare_and_fusion.4, ...), kind=kLoop, calls=%fused_computation.15.clone.1 | loop fusion | flops 5067776 | bytes 8693264 | tf_op jit(solution)/shard_map/while/body/eval_jaxpr/stack | solution.py:71
  110.1 2.3 fusion.67
  114.3 1.8 fusion.64
  117.9 1.9 slice.24
  119.8 3.6 %copy.36 = f32[1,1616,224,2]{1,2,3,0:T(8,128)} copy(f32[1,1616,224,2]{2,1,3,0:T(8,128)} %slice.24) | data formatting | bytes 5791744 | tf_op jit(solution)/shard_map/while
  123.4 1.9 slice.25
  125.3 3.8 %copy.37 = f32[1,1616,224,2]{1,2,3,0:T(8,128)} copy(f32[1,1616,224,2]{2,1,3,0:T(8,128)} %slice.25) | data formatting | bytes 5791744 | tf_op jit(solution)/shard_map/while
  129.1 2.7 %fusion.66 = (bf16[1616,224,2,1]{0,1,2,3:T(8,128)(2,1)S(1)}, bf16[1616,224,2,1]{0,1,2,3:T(8,128)(2,1)S(1)}) fusion(f32[1,1616,224,2]{1,2,3,0:T(8,128)S(1)} %copy-done.1, f32[224,2]{0,1:T(2,128)S(1)} %get-tuple-element.206, pred[1616]{0:T(1024)(128)(4,1)S(1)} %iota_compare_fusion.2, pred[224,2]{0,1:T(4,128)(4,1)S(1)} %compare_and_fusion.4, ...), kind=kLoop, calls=%fused_computation.15.clone.1 | loop fusion | flops 5067776 | bytes 8693264 | tf_op jit(solution)/shard_map/while/body/eval_jaxpr/stack | solution.py:71
  131.8 2.3 fusion.67
  136.0 1.8 fusion.64
  139.5 1.9 slice.24
  141.4 3.6 %copy.36 = f32[1,1616,224,2]{1,2,3,0:T(8,128)} copy(f32[1,1616,224,2]{2,1,3,0:T(8,128)} %slice.24) | data formatting | bytes 5791744 | tf_op jit(solution)/shard_map/while
  145.0 1.9 slice.25
  146.9 3.8 %copy.37 = f32[1,1616,224,2]{1,2,3,0:T(8,128)} copy(f32[1,1616,224,2]{2,1,3,0:T(8,128)} %slice.25) | data formatting | bytes 5791744 | tf_op jit(solution)/shard_map/while
  150.8 2.7 %fusion.66 = (bf16[1616,224,2,1]{0,1,2,3:T(8,128)(2,1)S(1)}, bf16[1616,224,2,1]{0,1,2,3:T(8,128)(2,1)S(1)}) fusion(f32[1,1616,224,2]{1,2,3,0:T(8,128)S(1)} %copy-done.1, f32[224,2]{0,1:T(2,128)S(1)} %get-tuple-element.206, pred[1616]{0:T(1024)(128)(4,1)S(1)} %iota_compare_fusion.2, pred[224,2]{0,1:T(4,128)(4,1)S(1)} %compare_and_fusion.4, ...), kind=kLoop, calls=%fused_computation.15.clone.1 | loop fusion | flops 5067776 | bytes 8693264 | tf_op jit(solution)/shard_map/while/body/eval_jaxpr/stack | solution.py:71
  153.4 2.3 fusion.67
  161.2 1.9 slice.24
  163.1 3.6 %copy.36 = f32[1,1616,224,2]{1,2,3,0:T(8,128)} copy(f32[1,1616,224,2]{2,1,3,0:T(8,128)} %slice.24) | data formatting | bytes 5791744 | tf_op jit(solution)/shard_map/while
  166.7 1.9 slice.25
  168.6 3.8 %copy.37 = f32[1,1616,224,2]{1,2,3,0:T(8,128)} copy(f32[1,1616,224,2]{2,1,3,0:T(8,128)} %slice.25) | data formatting | bytes 5791744 | tf_op jit(solution)/shard_map/while
  172.4 2.7 %fusion.66 = (bf16[1616,224,2,1]{0,1,2,3:T(8,128)(2,1)S(1)}, bf16[1616,224,2,1]{0,1,2,3:T(8,128)(2,1)S(1)}) fusion(f32[1,1616,224,2]{1,2,3,0:T(8,128)S(1)} %copy-done.1, f32[224,2]{0,1:T(2,128)S(1)} %get-tuple-element.206, pred[1616]{0:T(1024)(128)(4,1)S(1)} %iota_compare_fusion.2, pred[224,2]{0,1:T(4,128)(4,1)S(1)} %compare_and_fusion.4, ...), kind=kLoop, calls=%fused_computation.15.clone.1 | loop fusion | flops 5067776 | bytes 8693264 | tf_op jit(solution)/shard_map/while/body/eval_jaxpr/stack | solution.py:71
  175.1 2.3 fusion.67
  179.3 1.8 fusion.64
  182.8 1.9 slice.24
  184.7 3.6 %copy.36 = f32[1,1616,224,2]{1,2,3,0:T(8,128)} copy(f32[1,1616,224,2]{2,1,3,0:T(8,128)} %slice.24) | data formatting | bytes 5791744 | tf_op jit(solution)/shard_map/while
  188.3 1.9 slice.25
  190.2 3.8 %copy.37 = f32[1,1616,224,2]{1,2,3,0:T(8,128)} copy(f32[1,1616,224,2]{2,1,3,0:T(8,128)} %slice.25) | data formatting | bytes 5791744 | tf_op jit(solution)/shard_map/while
  194.1 2.7 %fusion.66 = (bf16[1616,224,2,1]{0,1,2,3:T(8,128)(2,1)S(1)}, bf16[1616,224,2,1]{0,1,2,3:T(8,128)(2,1)S(1)}) fusion(f32[1,1616,224,2]{1,2,3,0:T(8,128)S(1)} %copy-done.1, f32[224,2]{0,1:T(2,128)S(1)} %get-tuple-element.206, pred[1616]{0:T(1024)(128)(4,1)S(1)} %iota_compare_fusion.2, pred[224,2]{0,1:T(4,128)(4,1)S(1)} %compare_and_fusion.4, ...), kind=kLoop, calls=%fused_computation.15.clone.1 | loop fusion | flops 5067776 | bytes 8693264 | tf_op jit(solution)/shard_map/while/body/eval_jaxpr/stack | solution.py:71
  196.8 2.3 fusion.67
  200.9 1.8 fusion.64
  204.5 1.9 slice.24
  206.4 3.6 %copy.36 = f32[1,1616,224,2]{1,2,3,0:T(8,128)} copy(f32[1,1616,224,2]{2,1,3,0:T(8,128)} %slice.24) | data formatting | bytes 5791744 | tf_op jit(solution)/shard_map/while
  210.0 1.9 slice.25
  211.9 3.8 %copy.37 = f32[1,1616,224,2]{1,2,3,0:T(8,128)} copy(f32[1,1616,224,2]{2,1,3,0:T(8,128)} %slice.25) | data formatting | bytes 5791744 | tf_op jit(solution)/shard_map/while
  215.7 2.7 %fusion.66 = (bf16[1616,224,2,1]{0,1,2,3:T(8,128)(2,1)S(1)}, bf16[1616,224,2,1]{0,1,2,3:T(8,128)(2,1)S(1)}) fusion(f32[1,1616,224,2]{1,2,3,0:T(8,128)S(1)} %copy-done.1, f32[224,2]{0,1:T(2,128)S(1)} %get-tuple-element.206, pred[1616]{0:T(1024)(128)(4,1)S(1)} %iota_compare_fusion.2, pred[224,2]{0,1:T(4,128)(4,1)S(1)} %compare_and_fusion.4, ...), kind=kLoop, calls=%fused_computation.15.clone.1 | loop fusion | flops 5067776 | bytes 8693264 | tf_op jit(solution)/shard_map/while/body/eval_jaxpr/stack | solution.py:71
  218.4 2.3 fusion.67
  222.6 1.8 fusion.64
  226.2 1.9 slice.24
  228.1 3.6 %copy.36 = f32[1,1616,224,2]{1,2,3,0:T(8,128)} copy(f32[1,1616,224,2]{2,1,3,0:T(8,128)} %slice.24) | data formatting | bytes 5791744 | tf_op jit(solution)/shard_map/while
  231.7 1.9 slice.25
  233.6 3.8 %copy.37 = f32[1,1616,224,2]{1,2,3,0:T(8,128)} copy(f32[1,1616,224,2]{2,1,3,0:T(8,128)} %slice.25) | data formatting | bytes 5791744 | tf_op jit(solution)/shard_map/while
  237.4 2.7 %fusion.66 = (bf16[1616,224,2,1]{0,1,2,3:T(8,128)(2,1)S(1)}, bf16[1616,224,2,1]{0,1,2,3:T(8,128)(2,1)S(1)}) fusion(f32[1,1616,224,2]{1,2,3,0:T(8,128)S(1)} %copy-done.1, f32[224,2]{0,1:T(2,128)S(1)} %get-tuple-element.206, pred[1616]{0:T(1024)(128)(4,1)S(1)} %iota_compare_fusion.2, pred[224,2]{0,1:T(4,128)(4,1)S(1)} %compare_and_fusion.4, ...), kind=kLoop, calls=%fused_computation.15.clone.1 | loop fusion | flops 5067776 | bytes 8693264 | tf_op jit(solution)/shard_map/while/body/eval_jaxpr/stack | solution.py:71
  240.1 2.3 fusion.67
  247.8 1.9 slice.24
  249.7 3.6 %copy.36 = f32[1,1616,224,2]{1,2,3,0:T(8,128)} copy(f32[1,1616,224,2]{2,1,3,0:T(8,128)} %slice.24) | data formatting | bytes 5791744 | tf_op jit(solution)/shard_map/while
  253.3 1.9 slice.25
  255.2 3.8 %copy.37 = f32[1,1616,224,2]{1,2,3,0:T(8,128)} copy(f32[1,1616,224,2]{2,1,3,0:T(8,128)} %slice.25) | data formatting | bytes 5791744 | tf_op jit(solution)/shard_map/while
  259.1 2.7 %fusion.66 = (bf16[1616,224,2,1]{0,1,2,3:T(8,128)(2,1)S(1)}, bf16[1616,224,2,1]{0,1,2,3:T(8,128)(2,1)S(1)}) fusion(f32[1,1616,224,2]{1,2,3,0:T(8,128)S(1)} %copy-done.1, f32[224,2]{0,1:T(2,128)S(1)} %get-tuple-element.206, pred[1616]{0:T(1024)(128)(4,1)S(1)} %iota_compare_fusion.2, pred[224,2]{0,1:T(4,128)(4,1)S(1)} %compare_and_fusion.4, ...), kind=kLoop, calls=%fused_computation.15.clone.1 | loop fusion | flops 5067776 | bytes 8693264 | tf_op jit(solution)/shard_map/while/body/eval_jaxpr/stack | solution.py:71
  261.7 2.3 fusion.67
  (119 shorter events, 29.5 us)
Async XLA Ops:
  0.0 70.8 %copy-start = (s32[256]{0:T(256)S(1)}, s32[256]{0:T(256)}, u32[]{:S(2)}) copy-start(s32[256]{0:T(256)} %param.9) | copy-start | bytes 3076
  2.4 9.1 %copy-start.3 = (bf16[7,401,128]{2,1,0:T(8,128)(2,1)S(1)}, bf16[7,401,128]{2,1,0:T(8,128)(2,1)}, u32[]{:S(2)}) copy-start(bf16[7,401,128]{2,1,0:T(8,128)(2,1)} %param.6) | copy-start | bytes 2155780
  2.4 55.2 %all-to-all-start = ((bf16[8,7,401,32]{2,3,1,0:T(8,128)(2,1)}), bf16[8,7,401,32]{2,3,1,0:T(8,128)(2,1)S(1)}, u32[]{:S(2)}, u32[]{:S(2)}) async-start(bf16[8,7,401,32]{2,3,1,0:T(8,128)(2,1)} %broadcast_in_dim.98), calls=%async_computation | async-start | bytes 3670016 | tf_op jit(solution)/shard_map/all_to_all | solution.py:13
  13.0 3.6 %copy-start.4 = (s32[224]{0:T(256)S(1)}, s32[224]{0:T(256)}, u32[]{:S(2)}) copy-start(s32[224]{0:T(256)} %param.8) | copy-start | bytes 2692
  57.6 1.2 copy-start.2
  63.2 23.2 %all-to-all-start.1 = ((bf16[32,2,7168]{2,1,0:T(2,128)(2,1)}), bf16[32,2,7168]{2,1,0:T(2,128)(2,1)S(1)}, u32[]{:S(2)}, u32[]{:S(2)}) async-start(bf16[32,2,7168]{2,1,0:T(2,128)(2,1)} %reshape.588), calls=%async_computation.1 | async-start | bytes 1835008 | tf_op jit(solution)/shard_map/all_to_all | solution.py:102
  103.6 3.8 %copy-start.1 = (f32[1,1616,224,2]{1,2,3,0:T(8,128)S(1)}, f32[1,1616,224,2]{1,2,3,0:T(8,128)}, u32[]{:S(2)}) copy-start(f32[1,1616,224,2]{1,2,3,0:T(8,128)} %copy.36) | copy-start | bytes 8687620 | tf_op jit(solution)/shard_map/while
  125.3 3.8 %copy-start.1 = (f32[1,1616,224,2]{1,2,3,0:T(8,128)S(1)}, f32[1,1616,224,2]{1,2,3,0:T(8,128)}, u32[]{:S(2)}) copy-start(f32[1,1616,224,2]{1,2,3,0:T(8,128)} %copy.36) | copy-start | bytes 8687620 | tf_op jit(solution)/shard_map/while
  146.9 3.8 %copy-start.1 = (f32[1,1616,224,2]{1,2,3,0:T(8,128)S(1)}, f32[1,1616,224,2]{1,2,3,0:T(8,128)}, u32[]{:S(2)}) copy-start(f32[1,1616,224,2]{1,2,3,0:T(8,128)} %copy.36) | copy-start | bytes 8687620 | tf_op jit(solution)/shard_map/while
  168.6 3.8 %copy-start.1 = (f32[1,1616,224,2]{1,2,3,0:T(8,128)S(1)}, f32[1,1616,224,2]{1,2,3,0:T(8,128)}, u32[]{:S(2)}) copy-start(f32[1,1616,224,2]{1,2,3,0:T(8,128)} %copy.36) | copy-start | bytes 8687620 | tf_op jit(solution)/shard_map/while
  190.2 3.8 %copy-start.1 = (f32[1,1616,224,2]{1,2,3,0:T(8,128)S(1)}, f32[1,1616,224,2]{1,2,3,0:T(8,128)}, u32[]{:S(2)}) copy-start(f32[1,1616,224,2]{1,2,3,0:T(8,128)} %copy.36) | copy-start | bytes 8687620 | tf_op jit(solution)/shard_map/while
  211.9 3.8 %copy-start.1 = (f32[1,1616,224,2]{1,2,3,0:T(8,128)S(1)}, f32[1,1616,224,2]{1,2,3,0:T(8,128)}, u32[]{:S(2)}) copy-start(f32[1,1616,224,2]{1,2,3,0:T(8,128)} %copy.36) | copy-start | bytes 8687620 | tf_op jit(solution)/shard_map/while
  233.5 3.8 %copy-start.1 = (f32[1,1616,224,2]{1,2,3,0:T(8,128)S(1)}, f32[1,1616,224,2]{1,2,3,0:T(8,128)}, u32[]{:S(2)}) copy-start(f32[1,1616,224,2]{1,2,3,0:T(8,128)} %copy.36) | copy-start | bytes 8687620 | tf_op jit(solution)/shard_map/while
  255.2 3.8 %copy-start.1 = (f32[1,1616,224,2]{1,2,3,0:T(8,128)S(1)}, f32[1,1616,224,2]{1,2,3,0:T(8,128)}, u32[]{:S(2)}) copy-start(f32[1,1616,224,2]{1,2,3,0:T(8,128)} %copy.36) | copy-start | bytes 8687620 | tf_op jit(solution)/shard_map/while
where the time goes:
time: 265 us; the launch traced here: 264 us
  local copies, waits for them, and re-layouts  111 us (42%)
  waiting for transfers between devices  56.2 us (21%)
  other arithmetic  50.6 us (19%)
  matrix products  19.1 us (7%)
  starting transfers between devices  16.7 us (6%)
  loops' own time  10.5 us (4%)
    while x32, local copies, waits for them, and re-layouts  59.1 us
    all_to_all x1, waiting for transfers between devices, from_everyone(): return lax.all_to_all(copies, axis, split_axis=0, concat_axis=0, tiled=True)  40.7 us
    cos x16, other arithmetic, trig_parts(): return (jnp.cos(angles), jnp.sin(angles))  22.2 us
    another operation x8, other arithmetic, synthesis_table(): return jnp.stack([real_part, imag_part], axis=-1).astype(jnp.bfloat16)  21.4 us
    dot_general x8, matrix products, one_group(): jnp.einsum('rjghc,rghcl->rlj', basis, values, preferred_element_type=jnp....  18.4 us
    all_to_all x1, waiting for transfers between devices, on_device(): lax.all_to_all(fourier, 'wav', split_axis=0, concat_axis=1, tiled=True)  15.5 us
    slice x8, local copies, waits for them, and re-layouts, synthesis_table(): cos_all.reshape(row_total, coarse_count * 64, wave_numbers.shape[0], 2)  15.1 us
    slice x8, local copies, waits for them, and re-layouts, synthesis_table(): sin_all.reshape(row_total, coarse_count * 64, wave_numbers.shape[0], 2)  15.1 us
  transfers between devices with their start and end apart: 2, of which 2 were waited for; matrix products, arithmetic and copies ran while one was open for 2% of the time, Pallas kernels for 0%

commit v1 on v0

v1 whole, which is shorter than its diff:
```python
import functools
import math

import jax
import jax.numpy as jnp
import numpy as np
from jax import lax
from jax.experimental import pallas as pl
from jax.experimental.pallas import tpu as pltpu
from jax.sharding import PartitionSpec as P

NLAT = 800
WIDTH = 256
MESH = pl.DeviceIdType.MESH


def poly_in_square(fn, degree):
    nodes = np.cos(np.pi * (np.arange(200) + 0.5) / 200)
    top = 0.52**2
    z = (nodes + 1) * 0.5 * top
    fit = np.polynomial.chebyshev.Chebyshev.fit(z, fn(np.sqrt(z)), degree, domain=[0, top])
    return [float(c) for c in fit.convert(kind=np.polynomial.Polynomial).coef]


SIN_COEF = poly_in_square(lambda x: np.sin(np.pi * x) / x, 5)
COS_COEF = poly_in_square(lambda x: np.cos(np.pi * x), 5)


def horner(coef, z):
    acc = jnp.full_like(z, coef[-1])
    for c in coef[-2::-1]:
        acc = acc * z + c
    return acc


def half_angle(steps, count, inverse):
    turns = jnp.floor(steps * inverse + 0.5)
    x = (steps - turns * count) * inverse
    z = x * x
    return x * horner(SIN_COEF, z), horner(COS_COEF, z)


def exchange_kernel(
    slots, fold, tiles, batches, pair_ref, leg_ref, spec_ref, out_ref, held, rhs, ready, send_sem, recv_sem, out_send, out_recv, own_sem
):
    wav_count = lax.axis_size("wav")
    lev_count = lax.axis_size("lev")
    w = lax.axis_index("wav")
    z = lax.axis_index("lev")
    right = lax.rem(z + 1, lev_count)
    left = lax.rem(z + lev_count - 1, lev_count)
    block = leg_ref.shape[1]
    full = (fold // 128) * 128
    rest = fold - full
    per_slot = full // 128
    chunk = held.shape[2]

    barrier = pltpu.get_barrier_semaphore()
    for peer in (left, right):
        pl.semaphore_signal(barrier, inc=1, device_id={"lev": peer}, device_id_type=MESH)

    def greet(k, _):
        peer = lax.rem(w + k, wav_count)
        pl.semaphore_signal(barrier, inc=1, device_id={"wav": peer}, device_id_type=MESH)
        return 0

    lax.fori_loop(1, wav_count, greet, 0)

    tail = jnp.zeros((block, 128), jnp.float32)
    for s in range(slots):
        rows = lax.broadcasted_iota(jnp.int32, (rest, 128), 0)
        cols = lax.broadcasted_iota(jnp.int32, (rest, 128), 1)
        place = (cols == rows + rest * s).astype(jnp.bfloat16)
        tail += jnp.dot(leg_ref[s, :, full:fold], place, preferred_element_type=jnp.float32)
    held[z, 0, 0] = tail.astype(jnp.bfloat16)
    for s in range(slots):
        for k in range(per_slot):
            i = 1 + s * per_slot + k
            held[z, i // chunk, i % chunk] = leg_ref[s, :, k * 128 : (k + 1) * 128]

    pl.semaphore_wait(barrier, 2 + wav_count - 1)

    half = lev_count // 2

    def goes(side, d, c):
        return d < half - 1 or c % 2 == side

    def hop(side, d, c):
        owner = lax.rem(z + (lev_count - d if side == 0 else d), lev_count)
        return pltpu.make_async_remote_copy(
            src_ref=held.at[owner, c],
            dst_ref=held.at[owner, c],
            send_sem=send_sem.at[side, d, c],
            recv_sem=recv_sem.at[side, d, c],
            device_id={"lev": right if side == 0 else left},
            device_id_type=MESH,
        )

    def arrived(side, d, c):
        owner = lax.rem(z + (lev_count - d - 1 if side == 0 else d + 1), lev_count)
        pltpu.make_async_remote_copy(
            src_ref=held.at[owner, c],
            dst_ref=held.at[owner, c],
            send_sem=send_sem.at[side, d, c],
            recv_sem=recv_sem.at[side, d, c],
            device_id={"lev": right if side == 0 else left},
            device_id_type=MESH,
        ).wait_recv()

    def own(batch):
        for c in batch:
            for side in (0, 1):
                hop(side, 0, c).start()

    def forward(batch, d):
        for c in batch:
            for side in (0, 1):
                arrived(side, d - 1, c)
                if goes(side, d, c):
                    hop(side, d, c).start()

    landed = set()

    def last(c):
        if c not in landed:
            landed.add(c)
            arrived(c % 2, half - 1, c)

    def one_slot(s):
        parts = [0] + [1 + s * per_slot + k for k in range(per_slot)]
        for i in parts:
            last(i // chunk)
        total = None
        for a in range(0, len(parts), 2):
            pieces = [
                held[:, i // chunk, i % chunk].reshape(lev_count * block, 128) for i in parts[a : a + 2]
            ]
            lhs = jnp.concatenate(pieces, axis=1)
            term = jnp.dot(lhs, rhs[s, a * 128 : (a + 2) * 128], preferred_element_type=jnp.float32)
            total = term if total is None else total + term
        groups = total.reshape(wav_count, total.shape[0] // wav_count, 256)
        both = jnp.concatenate([groups[:, :, :128], groups[:, :, 128:]], axis=1)
        ready[s] = both.astype(jnp.bfloat16)

        def send(k, _):
            peer = lax.rem(w + k, wav_count)
            pltpu.make_async_remote_copy(
                src_ref=ready.at[s, peer],
                dst_ref=out_ref.at[w, s],
                send_sem=out_send,
                recv_sem=out_recv.at[w],
                device_id={"wav": peer},
                device_id_type=MESH,
            ).start()
            return 0

        lax.fori_loop(1, wav_count, send, 0)
        pltpu.make_async_copy(ready.at[s, w], out_ref.at[w, s], own_sem).start()

    own(batches[0])

    for s in range(slots):
        border = (fold - 1) - pair_ref[w * slots + s]
        rows = lax.broadcasted_iota(jnp.int32, (128, rest), 0)
        cols = lax.broadcasted_iota(jnp.int32, (128, rest), 1)
        place = (rows == cols + rest * s).astype(jnp.bfloat16)
        row = lax.broadcasted_iota(jnp.int32, (128, 128), 0)
        ending = jnp.dot(place, spec_ref[s, full:fold, :], preferred_element_type=jnp.float32)
        below = row - rest * s + full < border
        rhs[s, 0:128, 0:128] = jnp.where(below, ending, 0.0).astype(jnp.bfloat16)
        rhs[s, 0:128, 128:256] = jnp.where(below, 0.0, ending).astype(jnp.bfloat16)
        for k in range(per_slot):
            piece = spec_ref[s, k * 128 : (k + 1) * 128, :].astype(jnp.float32)
            below = row + k * 128 < border
            at = (k + 1) * 128
            rhs[s, at : at + 128, 0:128] = jnp.where(below, piece, 0.0).astype(jnp.bfloat16)
            rhs[s, at : at + 128, 128:256] = jnp.where(below, 0.0, piece).astype(jnp.bfloat16)

    todo = list(range(slots))
    for b, batch in enumerate(batches):
        if b:
            own(batch)
        seen = set(c for earlier in batches[:b] for c in earlier)
        for d in range(1, half):
            while b and todo:
                s = todo[0]
                if all((1 + s * per_slot + k) // chunk in seen for k in range(per_slot)):
                    one_slot(todo.pop(0))
                    break
                break
            forward(batch, d)
    for s in todo:
        one_slot(s)
    for c in range(held.shape[1]):
        last(c)

    for side in (0, 1):
        for d in range(half):
            for c in range(held.shape[1]):
                if goes(side, d, c):
                    hop(side, d, c).wait_send()

    def arrival(k, _):
        peer = lax.rem(w + k, wav_count)
        pltpu.make_async_copy(out_ref.at[peer], out_ref.at[peer], out_recv.at[peer]).wait()
        return 0

    lax.fori_loop(1, wav_count, arrival, 0)
    pltpu.make_async_copy(ready.at[:, 1:], ready.at[:, 1:], out_send).wait()
    pltpu.make_async_copy(out_ref.at[w], out_ref.at[w], own_sem).wait()


def exchange(spectral, legendre, wave_pair):
    slots, fold, _ = spectral.shape
    wav_count = lax.axis_size("wav")
    lev_count = lax.axis_size("lev")
    block = legendre.shape[2]
    rows = block * lev_count // wav_count
    turned = jnp.swapaxes(legendre, 1, 2)
    tiles = 1 + slots * (fold // 128)
    chunk = 2
    chunks = tiles // chunk
    batches = [list(range(6)), list(range(6, chunks))]
    half = lev_count // 2
    return pl.pallas_call(
        functools.partial(exchange_kernel, slots, fold, tiles, batches),
        out_shape=jax.ShapeDtypeStruct((wav_count, slots, 2 * rows, 128), jnp.bfloat16),
        in_specs=[
            pl.BlockSpec(memory_space=pltpu.SMEM),
            pl.BlockSpec(memory_space=pltpu.VMEM),
            pl.BlockSpec(memory_space=pltpu.VMEM),
        ],
        out_specs=pl.BlockSpec(memory_space=pl.ANY),
        scratch_shapes=[
            pltpu.VMEM((lev_count, chunks, chunk, block, 128), jnp.bfloat16),
            pltpu.VMEM((slots, 512, 256), jnp.bfloat16),
            pltpu.VMEM((slots, wav_count, 2 * rows, 128), jnp.bfloat16),
            pltpu.SemaphoreType.DMA((2, half, chunks)),
            pltpu.SemaphoreType.DMA((2, half, chunks)),
            pltpu.SemaphoreType.DMA,
            pltpu.SemaphoreType.DMA((wav_count,)),
            pltpu.SemaphoreType.DMA,
        ],
        compiler_params=pltpu.CompilerParams(collective_id=0, has_side_effects=True),
        name="exchange",
    )(wave_pair, turned, spectral)


def synthesis_kernel(waves, rows, pair_ref, lat_ref, in_ref, out_ref, flat, column, table, turned, half_turn):
    r = pl.program_id(0)
    slots = pair_ref.shape[1]
    layers = out_ref.shape[1]
    width = out_ref.shape[2]
    blocks = (width + WIDTH - 1) // WIDTH

    @pl.when(r == 0)
    def _():
        flat[...] = in_ref[...].astype(jnp.float32)
        pairs = pair_ref[...].astype(jnp.float32)
        column[...] = jnp.transpose(jnp.broadcast_to(pairs, (128, slots)))
        table[...] = jnp.zeros_like(table)
        turned[...] = jnp.zeros_like(turned)

    a = lat_ref[lax.axis_index("wav") * rows + r]
    lon = 20 + 4 * jnp.minimum(a, NLAT - 1 - a)
    highest = jnp.minimum(waves - 1, lax.shift_right_arithmetic(lon - 1, 1)).astype(jnp.float32)
    count = lon.astype(jnp.float32)
    count_col = jnp.full((slots, 128), count, jnp.float32)
    inverse_col = 1.0 / count_col
    lane = lax.broadcasted_iota(jnp.int32, (slots, 128), 1).astype(jnp.float32)

    for h in range(2):
        pair = column[...]
        m = pair if h == 0 else (waves - 1.0) - pair
        weight = jnp.where(m == 0.0, 1.0, 2.0)
        weight = jnp.where((pair >= 0.0) & (m <= highest), weight, 0.0)
        minus = -2.0 * weight
        for c in range(WIDTH // 128):
            sin_half, cos_half = half_angle(m * (lane + 128.0 * c), count_col, inverse_col)
            scaled = sin_half * minus
            at = pl.ds(h * 256, slots)
            table[at, c * 128 : (c + 1) * 128] = (weight + scaled * sin_half).astype(jnp.bfloat16)
            at = pl.ds(512 + h * 256, slots)
            table[at, c * 128 : (c + 1) * 128] = (scaled * cos_half).astype(jnp.bfloat16)

    target = lax.broadcasted_iota(jnp.int32, (128, 128), 0)
    source = lax.broadcasted_iota(jnp.int32, (128, 128), 1)
    part = (target >= layers).astype(jnp.int32)
    place = (source == 2 * (target - part * layers) + part).astype(jnp.bfloat16)
    count_row = jnp.full((8, slots), count, jnp.float32)
    inverse_row = 1.0 / count_row
    shift = lax.broadcasted_iota(jnp.int32, (8, slots), 0).astype(jnp.float32) * WIDTH
    for h in range(2):
        values = flat[pl.ds(h * rows + r, slots, stride=2 * rows), :].astype(jnp.bfloat16)
        split = lax.dot_general(
            place, values, (((1,), (1,)), ((), ())), preferred_element_type=jnp.float32
        )
        real, imag = split[:layers], split[layers:]
        pairs = jnp.broadcast_to(pair_ref[...].astype(jnp.float32), (8, slots))
        m = pairs if h == 0 else (waves - 1.0) - pairs
        sin_half, cos_half = half_angle(m * shift, count_row, inverse_row)
        sines = 2.0 * sin_half * cos_half
        cosines = 1.0 - 2.0 * sin_half * sin_half
        for b in range(blocks):
            at = pl.ds(b * layers, layers)
            if b == 0:
                turned_real, turned_imag = real, imag
            else:
                cos_b, sin_b = cosines[b : b + 1], sines[b : b + 1]
                turned_real = real * cos_b - imag * sin_b
                turned_imag = real * sin_b + imag * cos_b
            turned[at, h * 256 : h * 256 + slots] = turned_real.astype(jnp.bfloat16)
            turned[at, 512 + h * 256 : 512 + h * 256 + slots] = turned_imag.astype(jnp.bfloat16)

    result = jnp.dot(turned[...], table[...], preferred_element_type=jnp.float32)
    for b in range(blocks):
        size = min(WIDTH, width - b * WIDTH)
        col = lax.broadcasted_iota(jnp.int32, (layers, size), 1) + b * WIDTH
        piece = result[b * layers : (b + 1) * layers, :size]
        out_ref[0, :, b * WIDTH : b * WIDTH + size] = jnp.where(col < lon, piece, 0.0).astype(jnp.bfloat16)


def synthesis(received, wave_pair, lat_slot, waves):
    wav_count, slots, both, _ = received.shape
    rows = both // 2
    total = wav_count * slots
    layers = 64
    width = 2 * NLAT + 16
    blocks = (width + WIDTH - 1) // WIDTH
    flat = received.reshape(total * both, 128)
    return pl.pallas_call(
        functools.partial(synthesis_kernel, waves, rows),
        grid=(rows,),
        out_shape=jax.ShapeDtypeStruct((rows, layers, width), jnp.bfloat16),
        in_specs=[
            pl.BlockSpec((1, total), lambda r: (0, 0)),
            pl.BlockSpec(memory_space=pltpu.SMEM),
            pl.BlockSpec((total * both, 128), lambda r: (0, 0)),
        ],
        out_specs=pl.BlockSpec((1, layers, width), lambda r: (r, 0, 0)),
        scratch_shapes=[
            pltpu.VMEM((total * both, 128), jnp.float32),
            pltpu.VMEM((total, 128), jnp.float32),
            pltpu.VMEM((1024, WIDTH), jnp.bfloat16),
            pltpu.VMEM((blocks * layers, 1024), jnp.bfloat16),
            pltpu.VMEM((8, 128), jnp.float32),
        ],
        compiler_params=pltpu.CompilerParams(dimension_semantics=("arbitrary",)),
        name="synthesis",
    )(wave_pair.reshape(1, total), lat_slot, flat)


def on_device(spectral, legendre, wave_pair, lat_slot):
    received = exchange(spectral, legendre, wave_pair)
    return synthesis(received, wave_pair, lat_slot, spectral.shape[1] - 1)


def solution(mesh):
    return jax.shard_map(
        on_device,
        mesh=mesh,
        in_specs=(P("wav", None, "lev"), P("wav", None, "lev"), P(), P()),
        out_specs=P("wav", "lev", None),
        check_vma=False,
    )
```

time: 265 us -> 57.7 us (0.22)
  local copies, waits for them, and re-layouts: 111 us -> 0 us
  Pallas kernels: 0 us -> 57.6 us
  waiting for transfers between devices: 56.2 us -> 0 us
  other arithmetic: 50.6 us -> 0 us
  matrix products: 19.1 us -> 0 us
  starting transfers between devices: 16.7 us -> 0 us
  loops' own time: 10.5 us -> 0 us
    while x33 -> x0, local copies, waits for them, and re-layouts: 61.7 us -> none
    pallas_call x0 -> x2, Pallas kernels: none -> 57.6 us  [the longest x1 45.1 us: exchange(): pl.pallas_call(functools.partial(exchange_kernel, slots, fold, tiles, bat...]
    all_to_all x2 -> x0, waiting for transfers between devices: 56.2 us -> none  [the longest x1 40.7 us: from_everyone(): return lax.all_to_all(copies, axis, split_axis=0, concat_axis=0, tiled=True)]
    slice x16 -> x0, local copies, waits for them, and re-layouts: 30.3 us -> none  [the longest x8 15.1 us: synthesis_table(): cos_all.reshape(row_total, coarse_count * 64, wave_numbers.shape[0], 2)]
    cos x16 -> x0, other arithmetic: 22.2 us -> none  [trig_parts(): return (jnp.cos(angles), jnp.sin(angles))]
    another operation x17 -> x0, other arithmetic: 21.5 us -> none  [the longest x8 21.4 us: synthesis_table(): return jnp.stack([real_part, imag_part], axis=-1).astype(jnp.bfloat16)]
    dot_general x9 -> x0, matrix products: 19.1 us -> none  [the longest x8 18.4 us: one_group(): jnp.einsum('rjghc,rghcl->rlj', basis, values, preferred_element_type=jnp....]
    all_to_all x2 -> x0, starting transfers between devices: 16.7 us -> none  [the longest x1 9.13 us: from_everyone(): return lax.all_to_all(copies, axis, split_axis=0, concat_axis=0, tiled=True)]
  transfers between devices with their start and end apart: 2 -> 0, of which waited for: 2 -> 0; matrix products, arithmetic and copies ran while one was open for 2% -> 0% of each run, Pallas kernels for 0% -> 0%
where the time goes in v1:
time: 57.7 us; the launch traced here: 57.6 us
  Pallas kernels  57.6 us (100%)
    pallas_call x1, Pallas kernels, exchange(): pl.pallas_call(functools.partial(exchange_kernel, slots, fold, tiles, bat...  45.1 us
    pallas_call x1, Pallas kernels, synthesis(): pl.pallas_call(functools.partial(synthesis_kernel, waves, rows), grid=(ro...  12.5 us

profile of v1, /device:TPU:1, one launch (start us, length us, event | category | flops | bytes accessed | tf_op | source)
XLA Modules:
  0.0 57.6 jit_solution(15875775586892304561)
XLA Ops:
  0.0 45.1 %exchange.1 = bf16[32,7,16,128]{3,2,1,0:T(8,128)(2,1)} custom-call(s32[224]{0:T(256)} %pair_ref.1, bf16[7,32,401]{2,1,0:T(8,128)(2,1)} %bitcast.4, bf16[7,401,128]{2,1,0:T(8,128)(2,1)} %spec_ref.1), custom_call_target="tpu_custom_call" | custom-call | tf_op jit(solution)/shard_map/exchange/pallas_call | solution.py:225
  45.1 12.5 %synthesis.1 = bf16[8,64,1616]{2,1,0:T(8,128)(2,1)} custom-call(s32[1,224]{1,0:T(1,128)} %bitcast.5, s32[256]{0:T(256)} %lat_ref.1, bf16[3584,128]{1,0:T(8,128)(2,1)} %bitcast.3), custom_call_target="tpu_custom_call" | custom-call | tf_op jit(solution)/shard_map/synthesis/pallas_call | solution.py:331

commit v2 on v1

--- a/solution.py
+++ b/solution.py
@@ -1,5 +1,4 @@
 import functools
-import math
 
 import jax
 import jax.numpy as jnp
@@ -41,7 +40,34 @@
 
 
 def exchange_kernel(
-    slots, fold, tiles, batches, pair_ref, leg_ref, spec_ref, out_ref, held, rhs, ready, send_sem, recv_sem, out_send, out_recv, own_sem
+    waves,
+    slots,
+    fold,
+    order,
+    pair_hbm,
+    pairs_hbm,
+    lat_hbm,
+    leg_hbm,
+    spec_hbm,
+    out_ref,
+    table_hbm,
+    pair_ref,
+    pairs_ref,
+    lat_ref,
+    leg_ref,
+    spec_ref,
+    held,
+    rhs,
+    ready,
+    table,
+    column,
+    load_sem,
+    send_sem,
+    recv_sem,
+    out_send,
+    out_recv,
+    own_sem,
+    table_sem,
 ):
     wav_count = lax.axis_size("wav")
     lev_count = lax.axis_size("lev")
@@ -53,7 +79,15 @@
     full = (fold // 128) * 128
     rest = fold - full
     per_slot = full // 128
+    chunks = held.shape[1]
     chunk = held.shape[2]
+    rows = table.shape[0]
+    total_slots = column.shape[0]
+
+    sources = ((leg_hbm, leg_ref), (pair_hbm, pair_ref), (pairs_hbm, pairs_ref), (lat_hbm, lat_ref), (spec_hbm, spec_ref))
+    loads = [pltpu.make_async_copy(src, dst, load_sem.at[i]) for i, (src, dst) in enumerate(sources)]
+    for load in loads:
+        load.start()
 
     barrier = pltpu.get_barrier_semaphore()
     for peer in (left, right):
@@ -66,11 +100,12 @@
 
     lax.fori_loop(1, wav_count, greet, 0)
 
+    loads[0].wait()
     tail = jnp.zeros((block, 128), jnp.float32)
     for s in range(slots):
-        rows = lax.broadcasted_iota(jnp.int32, (rest, 128), 0)
-        cols = lax.broadcasted_iota(jnp.int32, (rest, 128), 1)
-        place = (cols == rows + rest * s).astype(jnp.bfloat16)
+        at_row = lax.broadcasted_iota(jnp.int32, (rest, 128), 0)
+        at_col = lax.broadcasted_iota(jnp.int32, (rest, 128), 1)
+        place = (at_col == at_row + rest * s).astype(jnp.bfloat16)
         tail += jnp.dot(leg_ref[s, :, full:fold], place, preferred_element_type=jnp.float32)
     held[z, 0, 0] = tail.astype(jnp.bfloat16)
     for s in range(slots):
@@ -107,17 +142,12 @@
             device_id_type=MESH,
         ).wait_recv()
 
-    def own(batch):
-        for c in batch:
-            for side in (0, 1):
-                hop(side, 0, c).start()
-
-    def forward(batch, d):
-        for c in batch:
-            for side in (0, 1):
+    def step(d, c):
+        for side in (0, 1):
+            if d:
                 arrived(side, d - 1, c)
-                if goes(side, d, c):
-                    hop(side, d, c).start()
+            if goes(side, d, c):
+                hop(side, d, c).start()
 
     landed = set()
 
@@ -125,6 +155,66 @@
         if c not in landed:
             landed.add(c)
             arrived(c % 2, half - 1, c)
+
+    def mask_slot(s):
+        border = (fold - 1) - pair_ref[w * slots + s]
+        at_row = lax.broadcasted_iota(jnp.int32, (128, rest), 0)
+        at_col = lax.broadcasted_iota(jnp.int32, (128, rest), 1)
+        place = (at_row == at_col + rest * s).astype(jnp.bfloat16)
+        row = lax.broadcasted_iota(jnp.int32, (128, 128), 0)
+        ending = jnp.dot(place, spec_ref[s, full:fold, :], preferred_element_type=jnp.float32)
+        below = row - rest * s + full < border
+        rhs[s, 0:128, 0:128] = jnp.where(below, ending, 0.0).astype(jnp.bfloat16)
+        rhs[s, 0:128, 128:256] = jnp.where(below, 0.0, ending).astype(jnp.bfloat16)
+        for k in range(per_slot):
+            piece = spec_ref[s, k * 128 : (k + 1) * 128, :].astype(jnp.float32)
+            below = row + k * 128 < border
+            at = (k + 1) * 128
+            rhs[s, at : at + 128, 0:128] = jnp.where(below, piece, 0.0).astype(jnp.bfloat16)
+            rhs[s, at : at + 128, 128:256] = jnp.where(below, 0.0, piece).astype(jnp.bfloat16)
+
+    def start_basis():
+        pairs = pairs_ref[...].astype(jnp.float32)
+        column[...] = jnp.transpose(jnp.broadcast_to(pairs, (128, total_slots)))
+        for r in range(rows):
+            for k in range(4):
+                at = k * 256 + total_slots
+                table[r, at : (k + 1) * 256, :] = jnp.zeros((256 - total_slots, WIDTH), jnp.bfloat16)
+
+    strip = 32
+    strips = total_slots // strip
+
+    def basis_piece(i, _):
+        r = lax.div(i, strips)
+        first = pl.multiple_of(lax.rem(i, strips) * strip, strip)
+        a = lat_ref[w * rows + r]
+        lon = 20 + 4 * jnp.minimum(a, NLAT - 1 - a)
+        highest = jnp.minimum(waves - 1, lax.shift_right_arithmetic(lon - 1, 1)).astype(jnp.float32)
+        count = jnp.full((strip, 128), lon.astype(jnp.float32), jnp.float32)
+        inverse = 1.0 / count
+        lane = lax.broadcasted_iota(jnp.int32, (strip, 128), 1).astype(jnp.float32)
+        pair = column[pl.ds(first, strip), :]
+        for h in range(2):
+            m = pair if h == 0 else (waves - 1.0) - pair
+            weight = jnp.where(m == 0.0, 1.0, 2.0)
+            weight = jnp.where((pair >= 0.0) & (m <= highest), weight, 0.0)
+            minus = -2.0 * weight
+            for c in range(WIDTH // 128):
+                sin_half, cos_half = half_angle(m * (lane + 128.0 * c), count, inverse)
+                scaled = sin_half * minus
+                cos_part = (weight + scaled * sin_half).astype(jnp.bfloat16)
+                sin_part = (scaled * cos_half).astype(jnp.bfloat16)
+                table[r, pl.ds(h * 256 + first, strip), c * 128 : (c + 1) * 128] = cos_part
+                table[r, pl.ds(512 + h * 256 + first, strip), c * 128 : (c + 1) * 128] = sin_part
+        return 0
+
+    made = [0]
+
+    def more_basis(n):
+        until = min(made[0] + n, rows * strips)
+        if until > made[0]:
+            lax.fori_loop(made[0], until, basis_piece, 0)
+            made[0] = until
 
     def one_slot(s):
         parts = [0] + [1 + s * per_slot + k for k in range(per_slot)]
@@ -157,48 +247,38 @@
         lax.fori_loop(1, wav_count, send, 0)
         pltpu.make_async_copy(ready.at[s, w], out_ref.at[w, s], own_sem).start()
 
-    own(batches[0])
-
-    for s in range(slots):
-        border = (fold - 1) - pair_ref[w * slots + s]
-        rows = lax.broadcasted_iota(jnp.int32, (128, rest), 0)
-        cols = lax.broadcasted_iota(jnp.int32, (128, rest), 1)
-        place = (rows == cols + rest * s).astype(jnp.bfloat16)
-        row = lax.broadcasted_iota(jnp.int32, (128, 128), 0)
-        ending = jnp.dot(place, spec_ref[s, full:fold, :], preferred_element_type=jnp.float32)
-        below = row - rest * s + full < border
-        rhs[s, 0:128, 0:128] = jnp.where(below, ending, 0.0).astype(jnp.bfloat16)
-        rhs[s, 0:128, 128:256] = jnp.where(below, 0.0, ending).astype(jnp.bfloat16)
-        for k in range(per_slot):
-            piece = spec_ref[s, k * 128 : (k + 1) * 128, :].astype(jnp.float32)
-            below = row + k * 128 < border
-            at = (k + 1) * 128
-            rhs[s, at : at + 128, 0:128] = jnp.where(below, piece, 0.0).astype(jnp.bfloat16)
-            rhs[s, at : at + 128, 128:256] = jnp.where(below, 0.0, piece).astype(jnp.bfloat16)
-
-    todo = list(range(slots))
-    for b, batch in enumerate(batches):
-        if b:
-            own(batch)
-        seen = set(c for earlier in batches[:b] for c in earlier)
-        for d in range(1, half):
-            while b and todo:
-                s = todo[0]
-                if all((1 + s * per_slot + k) // chunk in seen for k in range(per_slot)):
-                    one_slot(todo.pop(0))
-                    break
-                break
-            forward(batch, d)
-    for s in todo:
-        one_slot(s)
-    for c in range(held.shape[1]):
+    for entry in order:
+        kind, value = entry[0], entry[1:]
+        if kind == "hop":
+            step(*value)
+        elif kind == "slot":
+            one_slot(*value)
+        elif kind == "basis":
+            more_basis(*value)
+        elif kind == "mask":
+            loads[1].wait()
+            loads[4].wait()
+            for s in range(slots):
+                mask_slot(s)
+        else:
+            loads[2].wait()
+            loads[3].wait()
+            start_basis()
+    more_basis(rows * strips)
+    finish = pltpu.make_async_copy(table, table_hbm, table_sem)
+    finish.start()
+    for c in range(chunks):
         last(c)
 
     for side in (0, 1):
         for d in range(half):
-            for c in range(held.shape[1]):
+            for c in range(chunks):
                 if goes(side, d, c):
                     hop(side, d, c).wait_send()
+
+    finish.wait()
+    pltpu.make_async_copy(out_ref.at[w], out_ref.at[w], own_sem).wait()
+    pltpu.make_async_copy(ready.at[:, 1:], ready.at[:, 1:], out_send).wait()
 
     def arrival(k, _):
         peer = lax.rem(w + k, wav_count)
@@ -206,47 +286,85 @@
         return 0
 
     lax.fori_loop(1, wav_count, arrival, 0)
-    pltpu.make_async_copy(ready.at[:, 1:], ready.at[:, 1:], out_send).wait()
-    pltpu.make_async_copy(out_ref.at[w], out_ref.at[w], own_sem).wait()
-
-
-def exchange(spectral, legendre, wave_pair):
+
+
+def plan(chunks, slots):
+    early, late = list(range(5)), list(range(5, chunks))
+    order = []
+
+    def hops(d, which):
+        order.extend(("hop", d, c) for c in which)
+
+    hops(0, early)
+    hops(0, late[:3])
+    order.append(("mask",))
+    hops(1, early)
+    hops(0, late[3:])
+    order.append(("start",))
+    order.append(("basis", 12))
+    hops(2, early)
+    hops(1, late[:3])
+    order.append(("basis", 14))
+    hops(3, early)
+    hops(1, late[3:])
+    order.append(("basis", 16))
+    hops(2, late[:3])
+    order.append(("basis", 14))
+    order.append(("slot", 0))
+    hops(2, late[3:])
+    order.append(("slot", 1))
+    hops(3, late[:3])
+    order.append(("slot", 2))
+    hops(3, late[3:])
+    order.extend(("slot", s) for s in range(3, slots))
+    return order
+
+
+def exchange(spectral, legendre, wave_pair, lat_slot):
     slots, fold, _ = spectral.shape
     wav_count = lax.axis_size("wav")
     lev_count = lax.axis_size("lev")
     block = legendre.shape[2]
     rows = block * lev_count // wav_count
+    total = wave_pair.shape[0]
     turned = jnp.swapaxes(legendre, 1, 2)
     tiles = 1 + slots * (fold // 128)
     chunk = 2
     chunks = tiles // chunk
-    batches = [list(range(6)), list(range(6, chunks))]
     half = lev_count // 2
     return pl.pallas_call(
-        functools.partial(exchange_kernel, slots, fold, tiles, batches),
-        out_shape=jax.ShapeDtypeStruct((wav_count, slots, 2 * rows, 128), jnp.bfloat16),
-        in_specs=[
-            pl.BlockSpec(memory_space=pltpu.SMEM),
-            pl.BlockSpec(memory_space=pltpu.VMEM),
-            pl.BlockSpec(memory_space=pltpu.VMEM),
+        functools.partial(exchange_kernel, fold - 1, slots, fold, plan(chunks, slots)),
+        out_shape=[
+            jax.ShapeDtypeStruct((wav_count, slots, 2 * rows, 128), jnp.bfloat16),
+            jax.ShapeDtypeStruct((rows, 1024, WIDTH), jnp.bfloat16),
         ],
-        out_specs=pl.BlockSpec(memory_space=pl.ANY),
+        in_specs=[pl.BlockSpec(memory_space=pl.ANY)] * 5,
+        out_specs=[pl.BlockSpec(memory_space=pl.ANY)] * 2,
         scratch_shapes=[
+            pltpu.SMEM(wave_pair.shape, jnp.int32),
+            pltpu.VMEM((1, total), jnp.int32),
+            pltpu.SMEM(lat_slot.shape, jnp.int32),
+            pltpu.VMEM(turned.shape, jnp.bfloat16),
+            pltpu.VMEM(spectral.shape, jnp.bfloat16),
             pltpu.VMEM((lev_count, chunks, chunk, block, 128), jnp.bfloat16),
             pltpu.VMEM((slots, 512, 256), jnp.bfloat16),
             pltpu.VMEM((slots, wav_count, 2 * rows, 128), jnp.bfloat16),
+            pltpu.VMEM((rows, 1024, WIDTH), jnp.bfloat16),
+            pltpu.VMEM((total, 128), jnp.float32),
+            pltpu.SemaphoreType.DMA((5,)),
             pltpu.SemaphoreType.DMA((2, half, chunks)),
             pltpu.SemaphoreType.DMA((2, half, chunks)),
             pltpu.SemaphoreType.DMA,
             pltpu.SemaphoreType.DMA((wav_count,)),
             pltpu.SemaphoreType.DMA,
+            pltpu.SemaphoreType.DMA,
         ],
         compiler_params=pltpu.CompilerParams(collective_id=0, has_side_effects=True),
         name="exchange",
-    )(wave_pair, turned, spectral)
-
-
-def synthesis_kernel(waves, rows, pair_ref, lat_ref, in_ref, out_ref, flat, column, table, turned, half_turn):
+    )(wave_pair, wave_pair.reshape(1, total), lat_slot, turned, spectral)
+
+
+def synthesis_kernel(waves, rows, pair_ref, lat_ref, in_ref, table, out_ref, flat, turned):
     r = pl.program_id(0)
     slots = pair_ref.shape[1]
     layers = out_ref.shape[1]
@@ -256,33 +374,11 @@
     @pl.when(r == 0)
     def _():
         flat[...] = in_ref[...].astype(jnp.float32)
-        pairs = pair_ref[...].astype(jnp.float32)
-        column[...] = jnp.transpose(jnp.broadcast_to(pairs, (128, slots)))
-        table[...] = jnp.zeros_like(table)
         turned[...] = jnp.zeros_like(turned)
 
     a = lat_ref[lax.axis_index("wav") * rows + r]
     lon = 20 + 4 * jnp.minimum(a, NLAT - 1 - a)
-    highest = jnp.minimum(waves - 1, lax.shift_right_arithmetic(lon - 1, 1)).astype(jnp.float32)
     count = lon.astype(jnp.float32)
-    count_col = jnp.full((slots, 128), count, jnp.float32)
-    inverse_col = 1.0 / count_col
-    lane = lax.broadcasted_iota(jnp.int32, (slots, 128), 1).astype(jnp.float32)
-
-    for h in range(2):
-        pair = column[...]
-        m = pair if h == 0 else (waves - 1.0) - pair
-        weight = jnp.where(m == 0.0, 1.0, 2.0)
-        weight = jnp.where((pair >= 0.0) & (m <= highest), weight, 0.0)
-        minus = -2.0 * weight
-        for c in range(WIDTH // 128):
-            sin_half, cos_half = half_angle(m * (lane + 128.0 * c), count_col, inverse_col)
-            scaled = sin_half * minus
-            at = pl.ds(h * 256, slots)
-            table[at, c * 128 : (c + 1) * 128] = (weight + scaled * sin_half).astype(jnp.bfloat16)
-            at = pl.ds(512 + h * 256, slots)
-            table[at, c * 128 : (c + 1) * 128] = (scaled * cos_half).astype(jnp.bfloat16)
-
     target = lax.broadcasted_iota(jnp.int32, (128, 128), 0)
     source = lax.broadcasted_iota(jnp.int32, (128, 128), 1)
     part = (target >= layers).astype(jnp.int32)
@@ -312,7 +408,7 @@
             turned[at, h * 256 : h * 256 + slots] = turned_real.astype(jnp.bfloat16)
             turned[at, 512 + h * 256 : 512 + h * 256 + slots] = turned_imag.astype(jnp.bfloat16)
 
-    result = jnp.dot(turned[...], table[...], preferred_element_type=jnp.float32)
+    result = jnp.dot(turned[...], table[0], preferred_element_type=jnp.float32)
     for b in range(blocks):
         size = min(WIDTH, width - b * WIDTH)
         col = lax.broadcasted_iota(jnp.int32, (layers, size), 1) + b * WIDTH
@@ -320,7 +416,7 @@
         out_ref[0, :, b * WIDTH : b * WIDTH + size] = jnp.where(col < lon, piece, 0.0).astype(jnp.bfloat16)
 
 
-def synthesis(received, wave_pair, lat_slot, waves):
+def synthesis(received, table, wave_pair, lat_slot, waves):
     wav_count, slots, both, _ = received.shape
     rows = both // 2
     total = wav_count * slots
@@ -336,23 +432,21 @@
             pl.BlockSpec((1, total), lambda r: (0, 0)),
             pl.BlockSpec(memory_space=pltpu.SMEM),
             pl.BlockSpec((total * both, 128), lambda r: (0, 0)),
+            pl.BlockSpec((1, 1024, WIDTH), lambda r: (r, 0, 0)),
         ],
         out_specs=pl.BlockSpec((1, layers, width), lambda r: (r, 0, 0)),
         scratch_shapes=[
             pltpu.VMEM((total * both, 128), jnp.float32),
-            pltpu.VMEM((total, 128), jnp.float32),
-            pltpu.VMEM((1024, WIDTH), jnp.bfloat16),
             pltpu.VMEM((blocks * layers, 1024), jnp.bfloat16),
-            pltpu.VMEM((8, 128), jnp.float32),
         ],
         compiler_params=pltpu.CompilerParams(dimension_semantics=("arbitrary",)),
         name="synthesis",
-    )(wave_pair.reshape(1, total), lat_slot, flat)
+    )(wave_pair.reshape(1, total), lat_slot, flat, table)
 
 
 def on_device(spectral, legendre, wave_pair, lat_slot):
-    received = exchange(spectral, legendre, wave_pair)
-    return synthesis(received, wave_pair, lat_slot, spectral.shape[1] - 1)
+    received, table = exchange(spectral, legendre, wave_pair, lat_slot)
+    return synthesis(received, table, wave_pair, lat_slot, spectral.shape[1] - 1)
 
 
 def solution(mesh):

time: 57.7 us -> 48.8 us (0.85)
  Pallas kernels: 57.6 us -> 48.5 us
    pallas_call x1, Pallas kernels: 45.1 us -> 39.6 us  [exchange(): pl.pallas_call(functools.partial(exchange_kernel, fold - 1, slots, fold,...]
    pallas_call x1, Pallas kernels: 12.5 us -> 8.94 us  [synthesis(): pl.pallas_call(functools.partial(synthesis_kernel, waves, rows), grid=(ro...]
where the time goes in v2:
time: 48.8 us; the launch traced here: 48.5 us
  Pallas kernels  48.5 us (99%)
    pallas_call x1, Pallas kernels, exchange(): pl.pallas_call(functools.partial(exchange_kernel, fold - 1, slots, fold,...  39.6 us
    pallas_call x1, Pallas kernels, synthesis(): pl.pallas_call(functools.partial(synthesis_kernel, waves, rows), grid=(ro...  8.94 us

profile of v2, /device:TPU:1, one launch (start us, length us, event | category | flops | bytes accessed | tf_op | source)
XLA Modules:
  0.0 48.5 jit_solution(16368338764123707419)
XLA Ops:
  0.0 39.6 %exchange.1 = (bf16[32,7,16,128]{3,2,1,0:T(8,128)(2,1)}, bf16[8,1024,256]{2,1,0:T(8,128)(2,1)}) custom-call(s32[224]{0:T(256)} %pair_hbm.1, s32[1,224]{1,0:T(1,128)} %bitcast.5, s32[256]{0:T(256)} %lat_ref.1, bf16[7,32,401]{2,1,0:T(8,128)(2,1)} %bitcast.4, bf16[7,401,128]{2,1,0:T(8,128)(2,1)} %spec_hbm.1), custom_call_target="tpu_custom_call" | custom-call | tf_op jit(solution)/shard_map/exchange/pallas_call | solution.py:335
  39.6 8.9 %synthesis.1 = bf16[8,64,1616]{2,1,0:T(8,128)(2,1)} custom-call(s32[1,224]{1,0:T(1,128)} %bitcast.6, s32[256]{0:T(256)} %lat_ref.1, bf16[3584,128]{1,0:T(8,128)(2,1)} %bitcast.3, bf16[8,1024,256]{2,1,0:T(8,128)(2,1)} %get-tuple-element.8.table), custom_call_target="tpu_custom_call" | custom-call | tf_op jit(solution)/shard_map/synthesis/pallas_call | solution.py:427

commit v3 on v2

--- a/solution.py
+++ b/solution.py
@@ -10,6 +10,7 @@
 
 NLAT = 800
 WIDTH = 256
+PITCH = 24
 MESH = pl.DeviceIdType.MESH
 
 
@@ -179,7 +180,8 @@
         for r in range(rows):
             for k in range(4):
                 at = k * 256 + total_slots
-                table[r, at : (k + 1) * 256, :] = jnp.zeros((256 - total_slots, WIDTH), jnp.bfloat16)
+                for c in range(WIDTH // 128):
+                    table[r, c, at : (k + 1) * 256, :] = jnp.zeros((256 - total_slots, 128), jnp.bfloat16)
 
     strip = 32
     strips = total_slots // strip
@@ -204,8 +206,8 @@
                 scaled = sin_half * minus
                 cos_part = (weight + scaled * sin_half).astype(jnp.bfloat16)
                 sin_part = (scaled * cos_half).astype(jnp.bfloat16)
-                table[r, pl.ds(h * 256 + first, strip), c * 128 : (c + 1) * 128] = cos_part
-                table[r, pl.ds(512 + h * 256 + first, strip), c * 128 : (c + 1) * 128] = sin_part
+                table[r, c, pl.ds(h * 256 + first, strip), :] = cos_part
+                table[r, c, pl.ds(512 + h * 256 + first, strip), :] = sin_part
         return 0
 
     made = [0]
@@ -288,36 +290,19 @@
     lax.fori_loop(1, wav_count, arrival, 0)
 
 
-def plan(chunks, slots):
-    early, late = list(range(5)), list(range(5, chunks))
-    order = []
-
-    def hops(d, which):
-        order.extend(("hop", d, c) for c in which)
-
-    hops(0, early)
-    hops(0, late[:3])
-    order.append(("mask",))
-    hops(1, early)
-    hops(0, late[3:])
-    order.append(("start",))
-    order.append(("basis", 12))
-    hops(2, early)
-    hops(1, late[:3])
-    order.append(("basis", 14))
-    hops(3, early)
-    hops(1, late[3:])
-    order.append(("basis", 16))
-    hops(2, late[:3])
-    order.append(("basis", 14))
-    order.append(("slot", 0))
-    hops(2, late[3:])
-    order.append(("slot", 1))
-    hops(3, late[:3])
-    order.append(("slot", 2))
-    hops(3, late[3:])
-    order.extend(("slot", s) for s in range(3, slots))
-    return order
+def plan(slots):
+    hops = [(0, c) for c in (0, 1, 2, 3, 8, 5, 10, 4, 6, 9)]
+    order = [("hop", *hop) for hop in hops]
+    order += [("mask",), ("start",), ("basis", 20)]
+    later = [(1, 0), (1, 1), (1, 2), (0, 7), (1, 3), (1, 5), (1, 8), (1, 4), (1, 6), (1, 9), (2, 0), (2, 1)]
+    later += [(1, 10), (2, 2), (2, 3), (2, 5), (1, 7), (2, 4), (2, 6), (3, 0), (2, 8), (3, 1), (2, 10), (3, 2)]
+    later += [(2, 9), (3, 4), (3, 3), (3, 8), (3, 6), (2, 7), (3, 5)]
+    for i, hop in enumerate(later):
+        order.append(("hop", *hop))
+        if i % 3 == 2:
+            order.append(("basis", 4))
+    order += [("slot", 0), ("hop", 3, 10), ("slot", 1), ("hop", 3, 7), ("hop", 3, 9)]
+    return order + [("slot", s) for s in range(2, slots)]
 
 
 def exchange(spectral, legendre, wave_pair, lat_slot):
@@ -333,10 +318,10 @@
     chunks = tiles // chunk
     half = lev_count // 2
     return pl.pallas_call(
-        functools.partial(exchange_kernel, fold - 1, slots, fold, plan(chunks, slots)),
+        functools.partial(exchange_kernel, fold - 1, slots, fold, plan(slots)),
         out_shape=[
             jax.ShapeDtypeStruct((wav_count, slots, 2 * rows, 128), jnp.bfloat16),
-            jax.ShapeDtypeStruct((rows, 1024, WIDTH), jnp.bfloat16),
+            jax.ShapeDtypeStruct((rows, WIDTH // 128, 1024, 128), jnp.bfloat16),
         ],
         in_specs=[pl.BlockSpec(memory_space=pl.ANY)] * 5,
         out_specs=[pl.BlockSpec(memory_space=pl.ANY)] * 2,
@@ -349,7 +334,7 @@
             pltpu.VMEM((lev_count, chunks, chunk, block, 128), jnp.bfloat16),
             pltpu.VMEM((slots, 512, 256), jnp.bfloat16),
             pltpu.VMEM((slots, wav_count, 2 * rows, 128), jnp.bfloat16),
-            pltpu.VMEM((rows, 1024, WIDTH), jnp.bfloat16),
+            pltpu.VMEM((rows, WIDTH // 128, 1024, 128), jnp.bfloat16),
             pltpu.VMEM((total, 128), jnp.float32),
             pltpu.SemaphoreType.DMA((5,)),
             pltpu.SemaphoreType.DMA((2, half, chunks)),
@@ -364,56 +349,72 @@
     )(wave_pair, wave_pair.reshape(1, total), lat_slot, turned, spectral)
 
 
-def synthesis_kernel(waves, rows, pair_ref, lat_ref, in_ref, table, out_ref, flat, turned):
-    r = pl.program_id(0)
+def synthesis_kernel(waves, rows, together, pair_ref, lat_ref, in_ref, table, out_ref, flat, *turned):
+    step = pl.program_id(0)
     slots = pair_ref.shape[1]
     layers = out_ref.shape[1]
     width = out_ref.shape[2]
     blocks = (width + WIDTH - 1) // WIDTH
 
-    @pl.when(r == 0)
+    @pl.when(step == 0)
     def _():
-        flat[...] = in_ref[...].astype(jnp.float32)
-        turned[...] = jnp.zeros_like(turned)
-
-    a = lat_ref[lax.axis_index("wav") * rows + r]
-    lon = 20 + 4 * jnp.minimum(a, NLAT - 1 - a)
-    count = lon.astype(jnp.float32)
+        def unpack(i, _):
+            values = in_ref[pl.ds(pl.multiple_of(i * 2 * rows, 2 * rows), 2 * rows), :]
+            flat[pl.ds(pl.multiple_of(i * PITCH, 8), 2 * rows), :] = values.astype(jnp.float32)
+            return 0
+
+        lax.fori_loop(0, slots, unpack, 0, unroll=16)
+        for buffer in turned:
+            buffer[...] = jnp.zeros_like(buffer)
+
     target = lax.broadcasted_iota(jnp.int32, (128, 128), 0)
     source = lax.broadcasted_iota(jnp.int32, (128, 128), 1)
     part = (target >= layers).astype(jnp.int32)
     place = (source == 2 * (target - part * layers) + part).astype(jnp.bfloat16)
-    count_row = jnp.full((8, slots), count, jnp.float32)
-    inverse_row = 1.0 / count_row
     shift = lax.broadcasted_iota(jnp.int32, (8, slots), 0).astype(jnp.float32) * WIDTH
-    for h in range(2):
-        values = flat[pl.ds(h * rows + r, slots, stride=2 * rows), :].astype(jnp.bfloat16)
-        split = lax.dot_general(
-            place, values, (((1,), (1,)), ((), ())), preferred_element_type=jnp.float32
-        )
-        real, imag = split[:layers], split[layers:]
-        pairs = jnp.broadcast_to(pair_ref[...].astype(jnp.float32), (8, slots))
-        m = pairs if h == 0 else (waves - 1.0) - pairs
-        sin_half, cos_half = half_angle(m * shift, count_row, inverse_row)
-        sines = 2.0 * sin_half * cos_half
-        cosines = 1.0 - 2.0 * sin_half * sin_half
+    pairs = jnp.broadcast_to(pair_ref[...].astype(jnp.float32), (8, slots))
+    lengths = []
+    for i in range(together):
+        r = step * together + i
+        a = lat_ref[lax.axis_index("wav") * rows + r]
+        lon = 20 + 4 * jnp.minimum(a, NLAT - 1 - a)
+        lengths.append(lon)
+        count = jnp.full((8, slots), lon.astype(jnp.float32), jnp.float32)
+        inverse = 1.0 / count
+        for h in range(2):
+            values = flat[pl.ds(h * rows + r, slots, stride=PITCH), :].astype(jnp.bfloat16)
+            split = lax.dot_general(
+                place, values, (((1,), (1,)), ((), ())), preferred_element_type=jnp.float32
+            )
+            m = pairs if h == 0 else (waves - 1.0) - pairs
+            sin_half, cos_half = half_angle(m * shift, count, inverse)
+            sines = 2.0 * sin_half * cos_half
+            cosines = 1.0 - 2.0 * sin_half * sin_half
+            for k in range(2):
+                lanes = slice(k * 128, min((k + 1) * 128, slots))
+                size = lanes.stop - lanes.start
+                real, imag = split[:layers, lanes], split[layers:, lanes]
+                for b in range(blocks):
+                    at = pl.ds(b * layers, layers)
+                    if b == 0:
+                        turned_real, turned_imag = real, imag
+                    else:
+                        cos_b, sin_b = cosines[b : b + 1, lanes], sines[b : b + 1, lanes]
+                        turned_real = real * cos_b - imag * sin_b
+                        turned_imag = real * sin_b + imag * cos_b
+                    turned[i][2 * h + k, at, :size] = turned_real.astype(jnp.bfloat16)
+                    turned[i][4 + 2 * h + k, at, :size] = turned_imag.astype(jnp.bfloat16)
+
+    for i in range(together):
+        lhs = jnp.concatenate([turned[i][k] for k in range(8)], axis=1)
+        rhs = jnp.concatenate([table[i, c] for c in range(WIDTH // 128)], axis=1)
+        result = jnp.dot(lhs, rhs, preferred_element_type=jnp.float32)
         for b in range(blocks):
-            at = pl.ds(b * layers, layers)
-            if b == 0:
-                turned_real, turned_imag = real, imag
-            else:
-                cos_b, sin_b = cosines[b : b + 1], sines[b : b + 1]
-                turned_real = real * cos_b - imag * sin_b
-                turned_imag = real * sin_b + imag * cos_b
-            turned[at, h * 256 : h * 256 + slots] = turned_real.astype(jnp.bfloat16)
-            turned[at, 512 + h * 256 : 512 + h * 256 + slots] = turned_imag.astype(jnp.bfloat16)
-
-    result = jnp.dot(turned[...], table[0], preferred_element_type=jnp.float32)
-    for b in range(blocks):
-        size = min(WIDTH, width - b * WIDTH)
-        col = lax.broadcasted_iota(jnp.int32, (layers, size), 1) + b * WIDTH
-        piece = result[b * layers : (b + 1) * layers, :size]
-        out_ref[0, :, b * WIDTH : b * WIDTH + size] = jnp.where(col < lon, piece, 0.0).astype(jnp.bfloat16)
+            size = min(WIDTH, width - b * WIDTH)
+            col = lax.broadcasted_iota(jnp.int32, (layers, size), 1) + b * WIDTH
+            piece = result[b * layers : (b + 1) * layers, :size]
+            piece = jnp.where(col < lengths[i], piece, 0.0).astype(jnp.bfloat16)
+            out_ref[i, :, b * WIDTH : b * WIDTH + size] = piece
 
 
 def synthesis(received, table, wave_pair, lat_slot, waves):
@@ -423,22 +424,23 @@
     layers = 64
     width = 2 * NLAT + 16
     blocks = (width + WIDTH - 1) // WIDTH
+    together = 2
     flat = received.reshape(total * both, 128)
     return pl.pallas_call(
-        functools.partial(synthesis_kernel, waves, rows),
-        grid=(rows,),
+        functools.partial(synthesis_kernel, waves, rows, together),
+        grid=(rows // together,),
         out_shape=jax.ShapeDtypeStruct((rows, layers, width), jnp.bfloat16),
         in_specs=[
             pl.BlockSpec((1, total), lambda r: (0, 0)),
             pl.BlockSpec(memory_space=pltpu.SMEM),
             pl.BlockSpec((total * both, 128), lambda r: (0, 0)),
-            pl.BlockSpec((1, 1024, WIDTH), lambda r: (r, 0, 0)),
+            pl.BlockSpec((together, WIDTH // 128, 1024, 128), lambda r: (r, 0, 0, 0)),
         ],
-        out_specs=pl.BlockSpec((1, layers, width), lambda r: (r, 0, 0)),
+        out_specs=pl.BlockSpec((together, layers, width), lambda r: (r, 0, 0)),
         scratch_shapes=[
-            pltpu.VMEM((total * both, 128), jnp.float32),
-            pltpu.VMEM((blocks * layers, 1024), jnp.bfloat16),
-        ],
+            pltpu.VMEM((total * PITCH, 128), jnp.float32),
+        ]
+        + [pltpu.VMEM((8, blocks * layers, 128), jnp.bfloat16)] * together,
         compiler_params=pltpu.CompilerParams(dimension_semantics=("arbitrary",)),
         name="synthesis",
     )(wave_pair.reshape(1, total), lat_slot, flat, table)

time: 48.8 us -> 46.8 us (0.959)
  Pallas kernels: 48.5 us -> 46.7 us
    pallas_call x1, Pallas kernels: 8.94 us -> 7.12 us  [synthesis(): pl.pallas_call(functools.partial(synthesis_kernel, waves, rows, together)...]
where the time goes in v3:
time: 46.8 us; the launch traced here: 46.7 us
  Pallas kernels  46.7 us (100%)
    pallas_call x1, Pallas kernels, exchange(): pl.pallas_call(functools.partial(exchange_kernel, fold - 1, slots, fold,...  39.5 us
    pallas_call x1, Pallas kernels, synthesis(): pl.pallas_call(functools.partial(synthesis_kernel, waves, rows, together)...  7.12 us

profile of v3, /device:TPU:1, one launch (start us, length us, event | category | flops | bytes accessed | tf_op | source)
XLA Modules:
  0.0 46.7 jit_solution(5300773366208144676)
XLA Ops:
  0.0 39.5 %exchange.1 = (bf16[32,7,16,128]{3,2,1,0:T(8,128)(2,1)}, bf16[8,2,1024,128]{3,2,1,0:T(8,128)(2,1)}) custom-call(s32[224]{0:T(256)} %pair_hbm.1, s32[1,224]{1,0:T(1,128)} %bitcast.5, s32[256]{0:T(256)} %lat_ref.1, bf16[7,32,401]{2,1,0:T(8,128)(2,1)} %bitcast.4, bf16[7,401,128]{2,1,0:T(8,128)(2,1)} %spec_hbm.1), custom_call_target="tpu_custom_call" | custom-call | tf_op jit(solution)/shard_map/exchange/pallas_call | solution.py:320
  39.5 7.1 %synthesis.1 = bf16[8,64,1616]{2,1,0:T(8,128)(2,1)} custom-call(s32[1,224]{1,0:T(1,128)} %bitcast.6, s32[256]{0:T(256)} %lat_ref.1, bf16[3584,128]{1,0:T(8,128)(2,1)} %bitcast.3, bf16[8,2,1024,128]{3,2,1,0:T(8,128)(2,1)} %get-tuple-element.8.table), custom_call_target="tpu_custom_call" | custom-call | tf_op jit(solution)/shard_map/synthesis/pallas_call | solution.py:429

commit v4 on v3

--- a/solution.py
+++ b/solution.py
@@ -11,6 +11,7 @@
 NLAT = 800
 WIDTH = 256
 PITCH = 24
+GRANT = 20 * 2**20
 MESH = pl.DeviceIdType.MESH
 
 
@@ -51,7 +52,7 @@
     leg_hbm,
     spec_hbm,
     out_ref,
-    table_hbm,
+    table,
     pair_ref,
     pairs_ref,
     lat_ref,
@@ -60,15 +61,12 @@
     held,
     rhs,
     ready,
-    table,
     column,
     load_sem,
     send_sem,
     recv_sem,
     out_send,
     out_recv,
-    own_sem,
-    table_sem,
 ):
     wav_count = lax.axis_size("wav")
     lev_count = lax.axis_size("lev")
@@ -247,7 +245,7 @@
             return 0
 
         lax.fori_loop(1, wav_count, send, 0)
-        pltpu.make_async_copy(ready.at[s, w], out_ref.at[w, s], own_sem).start()
+        out_ref[w, s] = ready[s, w]
 
     for entry in order:
         kind, value = entry[0], entry[1:]
@@ -267,8 +265,6 @@
             loads[3].wait()
             start_basis()
     more_basis(rows * strips)
-    finish = pltpu.make_async_copy(table, table_hbm, table_sem)
-    finish.start()
     for c in range(chunks):
         last(c)
 
@@ -278,8 +274,6 @@
                 if goes(side, d, c):
                     hop(side, d, c).wait_send()
 
-    finish.wait()
-    pltpu.make_async_copy(out_ref.at[w], out_ref.at[w], own_sem).wait()
     pltpu.make_async_copy(ready.at[:, 1:], ready.at[:, 1:], out_send).wait()
 
     def arrival(k, _):
@@ -323,8 +317,8 @@
             jax.ShapeDtypeStruct((wav_count, slots, 2 * rows, 128), jnp.bfloat16),
             jax.ShapeDtypeStruct((rows, WIDTH // 128, 1024, 128), jnp.bfloat16),
         ],
-        in_specs=[pl.BlockSpec(memory_space=pl.ANY)] * 5,
-        out_specs=[pl.BlockSpec(memory_space=pl.ANY)] * 2,
+        in_specs=[pl.BlockSpec(memory_space=pltpu.HBM)] * 5,
+        out_specs=[pl.BlockSpec(memory_space=pltpu.VMEM)] * 2,
         scratch_shapes=[
             pltpu.SMEM(wave_pair.shape, jnp.int32),
             pltpu.VMEM((1, total), jnp.int32),
@@ -334,19 +328,18 @@
             pltpu.VMEM((lev_count, chunks, chunk, block, 128), jnp.bfloat16),
             pltpu.VMEM((slots, 512, 256), jnp.bfloat16),
             pltpu.VMEM((slots, wav_count, 2 * rows, 128), jnp.bfloat16),
-            pltpu.VMEM((rows, WIDTH // 128, 1024, 128), jnp.bfloat16),
             pltpu.VMEM((total, 128), jnp.float32),
             pltpu.SemaphoreType.DMA((5,)),
             pltpu.SemaphoreType.DMA((2, half, chunks)),
             pltpu.SemaphoreType.DMA((2, half, chunks)),
             pltpu.SemaphoreType.DMA,
             pltpu.SemaphoreType.DMA((wav_count,)),
-            pltpu.SemaphoreType.DMA,
-            pltpu.SemaphoreType.DMA,
         ],
-        compiler_params=pltpu.CompilerParams(collective_id=0, has_side_effects=True),
+        compiler_params=pltpu.CompilerParams(
+            collective_id=0, has_side_effects=True, vmem_limit_bytes=GRANT
+        ),
         name="exchange",
-    )(wave_pair, wave_pair.reshape(1, total), lat_slot, turned, spectral)
+    )(*(pltpu.with_memory_space_constraint(x, pltpu.HBM) for x in (wave_pair, wave_pair.reshape(1, total), lat_slot, turned, spectral)))
 
 
 def synthesis_kernel(waves, rows, together, pair_ref, lat_ref, in_ref, table, out_ref, flat, *turned):
@@ -441,7 +434,9 @@
             pltpu.VMEM((total * PITCH, 128), jnp.float32),
         ]
         + [pltpu.VMEM((8, blocks * layers, 128), jnp.bfloat16)] * together,
-        compiler_params=pltpu.CompilerParams(dimension_semantics=("arbitrary",)),
+        compiler_params=pltpu.CompilerParams(
+            dimension_semantics=("arbitrary",), vmem_limit_bytes=GRANT
+        ),
         name="synthesis",
     )(wave_pair.reshape(1, total), lat_slot, flat, table)
 

time: 46.8 us -> 46.6 us (level)
  Pallas kernels: 46.7 us -> 45.1 us
  local copies, waits for them, and re-layouts: 0 us -> 1.35 us
    pallas_call x1, Pallas kernels: 7.12 us -> 5.7 us  [synthesis(): pl.pallas_call(functools.partial(synthesis_kernel, waves, rows, together)...]
    unnamed x0 -> x4, local copies, waits for them, and re-layouts: none -> 1.35 us
where the time goes in v4:
time: 46.6 us; the launch traced here: 46.5 us
  Pallas kernels  45.1 us (97%)
  local copies, waits for them, and re-layouts  1.35 us (3%)
    pallas_call x1, Pallas kernels, exchange(): pl.pallas_call(functools.partial(exchange_kernel, fold - 1, slots, fold,...  39.4 us
    pallas_call x1, Pallas kernels, synthesis(): pl.pallas_call(functools.partial(synthesis_kernel, waves, rows, together)...  5.7 us
    unnamed x4, local copies, waits for them, and re-layouts  1.35 us

profile of v4, /device:TPU:1, one launch (start us, length us, event | category | flops | bytes accessed | tf_op | source)
XLA Modules:
  0.0 46.5 jit_solution(2985606938899248503)
XLA Ops:
  0.0 39.4 %exchange.1 = (bf16[32,7,16,128]{3,2,1,0:T(8,128)(2,1)S(1)}, bf16[8,2,1024,128]{3,2,1,0:T(8,128)(2,1)S(1)}) custom-call(s32[224]{0:T(256)} %pair_hbm.1, s32[1,224]{1,0:T(1,128)} %bitcast.4, s32[256]{0:T(256)} %lat_ref.1, bf16[7,32,401]{2,1,0:T(8,128)(2,1)} %bitcast.6, bf16[7,401,128]{2,1,0:T(8,128)(2,1)} %spec_hbm.1), custom_call_target="tpu_custom_call" | custom-call | tf_op jit(solution)/shard_map/exchange/pallas_call | solution.py:314
  39.4 0.0 copy-start
  39.4 0.7 %copy-done = s32[224]{0:T(256)S(1)} copy-done((s32[224]{0:T(256)S(1)}, s32[224]{0:T(256)}, u32[]{:S(2)}) %copy-start) | copy-done | bytes 920
  40.1 0.0 copy-start.1
  40.1 0.7 %copy-done.1 = s32[256]{0:T(256)S(1)} copy-done((s32[256]{0:T(256)S(1)}, s32[256]{0:T(256)}, u32[]{:S(2)}) %copy-start.1) | copy-done | bytes 1048
  40.8 5.7 %synthesis.1 = bf16[8,64,1616]{2,1,0:T(8,128)(2,1)} custom-call(s32[1,224]{1,0:T(1,128)S(1)} %bitcast.5, s32[256]{0:T(256)S(1)} %copy-done.1, bf16[3584,128]{1,0:T(8,128)(2,1)S(1)} %bitcast.3, bf16[8,2,1024,128]{3,2,1,0:T(8,128)(2,1)S(1)} %get-tuple-element.8.table), custom_call_target="tpu_custom_call" | custom-call | tf_op jit(solution)/shard_map/synthesis/pallas_call | solution.py:422
Async XLA Ops:
  39.4 0.7 %copy-start = (s32[224]{0:T(256)S(1)}, s32[224]{0:T(256)}, u32[]{:S(2)}) copy-start(s32[224]{0:T(256)} %pair_hbm.1) | copy-start | bytes 2692
  40.1 0.7 %copy-start.1 = (s32[256]{0:T(256)S(1)}, s32[256]{0:T(256)}, u32[]{:S(2)}) copy-start(s32[256]{0:T(256)} %lat_ref.1) | copy-start | bytes 3076

commit v5 on v4

--- a/solution.py
+++ b/solution.py
@@ -11,6 +11,7 @@
 NLAT = 800
 WIDTH = 256
 PITCH = 24
+EARLY = 3
 GRANT = 20 * 2**20
 MESH = pl.DeviceIdType.MESH
 
@@ -39,6 +40,62 @@
     x = (steps - turns * count) * inverse
     z = x * x
     return x * horner(SIN_COEF, z), horner(COS_COEF, z)
+
+
+def lined_up(pairs, first, past, wav_count, slots):
+    lanes = 4 * wav_count
+    index = lax.broadcasted_iota(jnp.int32, (pairs.shape[1], lanes), 0)
+    lane = lax.broadcasted_iota(jnp.int32, (pairs.shape[1], lanes), 1)
+    local = first + lax.div(lane, wav_count)
+    chosen = (index == lax.rem(lane, wav_count) * slots + local) & (local < past)
+    shifted = jnp.broadcast_to(pairs + 1.0, (16, pairs.shape[1])).astype(jnp.bfloat16)
+    return jnp.dot(shifted, chosen.astype(jnp.bfloat16), preferred_element_type=jnp.float32)[:8] - 1.0
+
+
+def unpack(flat, source, count, both):
+    def piece(i, _):
+        values = source[pl.ds(pl.multiple_of(i * both, both), both), :]
+        flat[pl.ds(pl.multiple_of(i * PITCH, 8), both), :] = values.astype(jnp.float32)
+        return 0
+
+    lax.fori_loop(0, count, piece, 0, unroll=16)
+
+
+def turn_row(waves, rows, layers, blocks, count, pairs, flat, r, lon, turned):
+    target = lax.broadcasted_iota(jnp.int32, (128, 128), 0)
+    source = lax.broadcasted_iota(jnp.int32, (128, 128), 1)
+    part = (target >= layers).astype(jnp.int32)
+    place = (source == 2 * (target - part * layers) + part).astype(jnp.bfloat16)
+    shift = lax.broadcasted_iota(jnp.int32, (8, count), 0).astype(jnp.float32) * WIDTH
+    points = jnp.full((8, count), lon.astype(jnp.float32), jnp.float32)
+    inverse = 1.0 / points
+    for h in range(2):
+        values = flat[pl.ds(h * rows + r, count, stride=PITCH), :].astype(jnp.bfloat16)
+        split = lax.dot_general(place, values, (((1,), (1,)), ((), ())), preferred_element_type=jnp.float32)
+        real, imag = split[:layers], split[layers:]
+        m = pairs[:, :count] if h == 0 else (waves - 1.0) - pairs[:, :count]
+        sin_half, cos_half = half_angle(m * shift, points, inverse)
+        sines = 2.0 * sin_half * cos_half
+        cosines = 1.0 - 2.0 * sin_half * sin_half
+        for b in range(blocks):
+            at = pl.ds(b * layers, layers)
+            if b == 0:
+                turned_real, turned_imag = real, imag
+            else:
+                cos_b, sin_b = cosines[b : b + 1], sines[b : b + 1]
+                turned_real = real * cos_b - imag * sin_b
+                turned_imag = real * sin_b + imag * cos_b
+            turned[h, at, :count] = turned_real.astype(jnp.bfloat16)
+            turned[2 + h, at, :count] = turned_imag.astype(jnp.bfloat16)
+
+
+def multiply(turned, columns):
+    lhs = jnp.concatenate([turned[k] for k in range(4)], axis=1)
+    return jnp.dot(lhs, jnp.concatenate(columns, axis=1), preferred_element_type=jnp.float32)
+
+
+def longitudes(latitude):
+    return 20 + 4 * jnp.minimum(latitude, NLAT - 1 - latitude)
 
 
 def exchange_kernel(
@@ -51,8 +108,9 @@
     lat_hbm,
     leg_hbm,
     spec_hbm,
-    out_ref,
+    late_ref,
     table,
+    sums,
     pair_ref,
     pairs_ref,
     lat_ref,
@@ -62,6 +120,10 @@
     rhs,
     ready,
     column,
+    lanes,
+    early,
+    flat,
+    turned,
     load_sem,
     send_sem,
     recv_sem,
@@ -80,7 +142,7 @@
     per_slot = full // 128
     chunks = held.shape[1]
     chunk = held.shape[2]
-    rows = table.shape[0]
+    rows = table.shape[1]
     total_slots = column.shape[0]
 
     sources = ((leg_hbm, leg_ref), (pair_hbm, pair_ref), (pairs_hbm, pairs_ref), (lat_hbm, lat_ref), (spec_hbm, spec_ref))
@@ -174,21 +236,21 @@
 
     def start_basis():
         pairs = pairs_ref[...].astype(jnp.float32)
-        column[...] = jnp.transpose(jnp.broadcast_to(pairs, (128, total_slots)))
-        for r in range(rows):
-            for k in range(4):
-                at = k * 256 + total_slots
-                for c in range(WIDTH // 128):
-                    table[r, c, at : (k + 1) * 256, :] = jnp.zeros((256 - total_slots, 128), jnp.bfloat16)
+        for g in range(2):
+            lined = lined_up(pairs, EARLY * g, slots if g else EARLY, wav_count, slots)
+            lanes[:, g * 128 : (g + 1) * 128] = lined
+            column[g * 128 : (g + 1) * 128, :] = jnp.transpose(jnp.broadcast_to(lined[:1], (128, 128)))
 
     strip = 32
     strips = total_slots // strip
 
     def basis_piece(i, _):
         r = lax.div(i, strips)
-        first = pl.multiple_of(lax.rem(i, strips) * strip, strip)
-        a = lat_ref[w * rows + r]
-        lon = 20 + 4 * jnp.minimum(a, NLAT - 1 - a)
+        block_of = lax.rem(i, strips)
+        first = pl.multiple_of(block_of * strip, strip)
+        group = lax.div(block_of, 4)
+        local = pl.multiple_of(lax.rem(block_of, 4) * strip, strip)
+        lon = longitudes(lat_ref[w * rows + r])
         highest = jnp.minimum(waves - 1, lax.shift_right_arithmetic(lon - 1, 1)).astype(jnp.float32)
         count = jnp.full((strip, 128), lon.astype(jnp.float32), jnp.float32)
         inverse = 1.0 / count
@@ -204,8 +266,8 @@
                 scaled = sin_half * minus
                 cos_part = (weight + scaled * sin_half).astype(jnp.bfloat16)
                 sin_part = (scaled * cos_half).astype(jnp.bfloat16)
-                table[r, c, pl.ds(h * 256 + first, strip), :] = cos_part
-                table[r, c, pl.ds(512 + h * 256 + first, strip), :] = sin_part
+                table[group, r, c, pl.ds(h * 128 + local, strip), :] = cos_part
+                table[group, r, c, pl.ds(256 + h * 128 + local, strip), :] = sin_part
         return 0
 
     made = [0]
@@ -232,20 +294,25 @@
         both = jnp.concatenate([groups[:, :, :128], groups[:, :, 128:]], axis=1)
         ready[s] = both.astype(jnp.bfloat16)
 
+        place = early.at[s, w] if s < EARLY else late_ref.at[s - EARLY, w]
+
         def send(k, _):
             peer = lax.rem(w + k, wav_count)
             pltpu.make_async_remote_copy(
                 src_ref=ready.at[s, peer],
-                dst_ref=out_ref.at[w, s],
+                dst_ref=place,
                 send_sem=out_send,
-                recv_sem=out_recv.at[w],
+                recv_sem=out_recv.at[s],
                 device_id={"wav": peer},
                 device_id_type=MESH,
             ).start()
             return 0
 
         lax.fori_loop(1, wav_count, send, 0)
-        out_ref[w, s] = ready[s, w]
+        if s < EARLY:
+            early[s, w] = ready[s, w]
+        else:
+            late_ref[s - EARLY, w] = ready[s, w]
 
     for entry in order:
         kind, value = entry[0], entry[1:]
@@ -268,6 +335,26 @@
     for c in range(chunks):
         last(c)
 
+    def arrival(s):
+        target = early.at[s, 1:] if s < EARLY else late_ref.at[s - EARLY, 1:]
+        pltpu.make_async_copy(target, target, out_recv.at[s]).wait()
+
+    for s in range(EARLY):
+        arrival(s)
+    both = early.shape[2]
+    for s in range(EARLY):
+        unpack(flat.at[pl.ds(s * wav_count * PITCH, wav_count * PITCH)], early.at[s].reshape(wav_count * both, 128), wav_count, both)
+
+    turned[...] = jnp.zeros_like(turned)
+
+    def one_row(r, _):
+        lon = longitudes(lat_ref[w * rows + r])
+        turn_row(waves, rows, 64, sums.shape[1] // 64, EARLY * wav_count, lanes[:, :128], flat, r, lon, turned)
+        sums[r] = multiply(turned, [table[0, r, c] for c in range(WIDTH // 128)])
+        return 0
+
+    lax.fori_loop(0, rows, one_row, 0)
+
     for side in (0, 1):
         for d in range(half):
             for c in range(chunks):
@@ -275,19 +362,14 @@
                     hop(side, d, c).wait_send()
 
     pltpu.make_async_copy(ready.at[:, 1:], ready.at[:, 1:], out_send).wait()
-
-    def arrival(k, _):
-        peer = lax.rem(w + k, wav_count)
-        pltpu.make_async_copy(out_ref.at[peer], out_ref.at[peer], out_recv.at[peer]).wait()
-        return 0
-
-    lax.fori_loop(1, wav_count, arrival, 0)
+    for s in range(EARLY, slots):
+        arrival(s)
 
 
 def plan(slots):
     hops = [(0, c) for c in (0, 1, 2, 3, 8, 5, 10, 4, 6, 9)]
     order = [("hop", *hop) for hop in hops]
-    order += [("mask",), ("start",), ("basis", 20)]
+    order += [("mask",), ("start",), ("basis", 24)]
     later = [(1, 0), (1, 1), (1, 2), (0, 7), (1, 3), (1, 5), (1, 8), (1, 4), (1, 6), (1, 9), (2, 0), (2, 1)]
     later += [(1, 10), (2, 2), (2, 3), (2, 5), (1, 7), (2, 4), (2, 6), (3, 0), (2, 8), (3, 1), (2, 10), (3, 2)]
     later += [(2, 9), (3, 4), (3, 3), (3, 8), (3, 6), (2, 7), (3, 5)]
@@ -311,14 +393,16 @@
     chunk = 2
     chunks = tiles // chunk
     half = lev_count // 2
+    moved = (2 * NLAT + 16 + WIDTH - 1) // WIDTH * 64
     return pl.pallas_call(
         functools.partial(exchange_kernel, fold - 1, slots, fold, plan(slots)),
         out_shape=[
-            jax.ShapeDtypeStruct((wav_count, slots, 2 * rows, 128), jnp.bfloat16),
-            jax.ShapeDtypeStruct((rows, WIDTH // 128, 1024, 128), jnp.bfloat16),
+            jax.ShapeDtypeStruct((slots - EARLY, wav_count, 2 * rows, 128), jnp.bfloat16),
+            jax.ShapeDtypeStruct((2, rows, WIDTH // 128, 512, 128), jnp.bfloat16),
+            jax.ShapeDtypeStruct((rows, moved, WIDTH), jnp.float32),
         ],
-        in_specs=[pl.BlockSpec(memory_space=pltpu.HBM)] * 5,
-        out_specs=[pl.BlockSpec(memory_space=pltpu.VMEM)] * 2,
+        in_specs=[pl.BlockSpec(memory_space=pl.ANY)] * 5,
+        out_specs=[pl.BlockSpec(memory_space=pltpu.VMEM)] * 3,
         scratch_shapes=[
             pltpu.SMEM(wave_pair.shape, jnp.int32),
             pltpu.VMEM((1, total), jnp.int32),
@@ -328,12 +412,16 @@
             pltpu.VMEM((lev_count, chunks, chunk, block, 128), jnp.bfloat16),
             pltpu.VMEM((slots, 512, 256), jnp.bfloat16),
             pltpu.VMEM((slots, wav_count, 2 * rows, 128), jnp.bfloat16),
-            pltpu.VMEM((total, 128), jnp.float32),
+            pltpu.VMEM((256, 128), jnp.float32),
+            pltpu.VMEM((8, 256), jnp.float32),
+            pltpu.VMEM((EARLY, wav_count, 2 * rows, 128), jnp.bfloat16),
+            pltpu.VMEM((EARLY * wav_count * PITCH, 128), jnp.float32),
+            pltpu.VMEM((4, moved, 128), jnp.bfloat16),
             pltpu.SemaphoreType.DMA((5,)),
             pltpu.SemaphoreType.DMA((2, half, chunks)),
             pltpu.SemaphoreType.DMA((2, half, chunks)),
             pltpu.SemaphoreType.DMA,
-            pltpu.SemaphoreType.DMA((wav_count,)),
+            pltpu.SemaphoreType.DMA((slots,)),
         ],
         compiler_params=pltpu.CompilerParams(
             collective_id=0, has_side_effects=True, vmem_limit_bytes=GRANT
@@ -342,66 +430,28 @@
     )(*(pltpu.with_memory_space_constraint(x, pltpu.HBM) for x in (wave_pair, wave_pair.reshape(1, total), lat_slot, turned, spectral)))
 
 
-def synthesis_kernel(waves, rows, together, pair_ref, lat_ref, in_ref, table, out_ref, flat, *turned):
+def synthesis_kernel(waves, rows, together, slots, pair_ref, lat_ref, in_ref, table, sums, out_ref, flat, lanes, *turned):
     step = pl.program_id(0)
-    slots = pair_ref.shape[1]
     layers = out_ref.shape[1]
     width = out_ref.shape[2]
     blocks = (width + WIDTH - 1) // WIDTH
+    count = in_ref.shape[0] // (2 * rows)
 
     @pl.when(step == 0)
     def _():
-        def unpack(i, _):
-            values = in_ref[pl.ds(pl.multiple_of(i * 2 * rows, 2 * rows), 2 * rows), :]
-            flat[pl.ds(pl.multiple_of(i * PITCH, 8), 2 * rows), :] = values.astype(jnp.float32)
-            return 0
-
-        lax.fori_loop(0, slots, unpack, 0, unroll=16)
+        unpack(flat, in_ref, count, 2 * rows)
+        lanes[...] = lined_up(pair_ref[...].astype(jnp.float32), EARLY, slots, lax.axis_size("wav"), slots)
         for buffer in turned:
             buffer[...] = jnp.zeros_like(buffer)
 
-    target = lax.broadcasted_iota(jnp.int32, (128, 128), 0)
-    source = lax.broadcasted_iota(jnp.int32, (128, 128), 1)
-    part = (target >= layers).astype(jnp.int32)
-    place = (source == 2 * (target - part * layers) + part).astype(jnp.bfloat16)
-    shift = lax.broadcasted_iota(jnp.int32, (8, slots), 0).astype(jnp.float32) * WIDTH
-    pairs = jnp.broadcast_to(pair_ref[...].astype(jnp.float32), (8, slots))
     lengths = []
     for i in range(together):
         r = step * together + i
-        a = lat_ref[lax.axis_index("wav") * rows + r]
-        lon = 20 + 4 * jnp.minimum(a, NLAT - 1 - a)
-        lengths.append(lon)
-        count = jnp.full((8, slots), lon.astype(jnp.float32), jnp.float32)
-        inverse = 1.0 / count
-        for h in range(2):
-            values = flat[pl.ds(h * rows + r, slots, stride=PITCH), :].astype(jnp.bfloat16)
-            split = lax.dot_general(
-                place, values, (((1,), (1,)), ((), ())), preferred_element_type=jnp.float32
-            )
-            m = pairs if h == 0 else (waves - 1.0) - pairs
-            sin_half, cos_half = half_angle(m * shift, count, inverse)
-            sines = 2.0 * sin_half * cos_half
-            cosines = 1.0 - 2.0 * sin_half * sin_half
-            for k in range(2):
-                lanes = slice(k * 128, min((k + 1) * 128, slots))
-                size = lanes.stop - lanes.start
-                real, imag = split[:layers, lanes], split[layers:, lanes]
-                for b in range(blocks):
-                    at = pl.ds(b * layers, layers)
-                    if b == 0:
-                        turned_real, turned_imag = real, imag
-                    else:
-                        cos_b, sin_b = cosines[b : b + 1, lanes], sines[b : b + 1, lanes]
-                        turned_real = real * cos_b - imag * sin_b
-                        turned_imag = real * sin_b + imag * cos_b
-                    turned[i][2 * h + k, at, :size] = turned_real.astype(jnp.bfloat16)
-                    turned[i][4 + 2 * h + k, at, :size] = turned_imag.astype(jnp.bfloat16)
+        lengths.append(longitudes(lat_ref[lax.axis_index("wav") * rows + r]))
+        turn_row(waves, rows, layers, blocks, count, lanes[...], flat, r, lengths[i], turned[i])
 
     for i in range(together):
-        lhs = jnp.concatenate([turned[i][k] for k in range(8)], axis=1)
-        rhs = jnp.concatenate([table[i, c] for c in range(WIDTH // 128)], axis=1)
-        result = jnp.dot(lhs, rhs, preferred_element_type=jnp.float32)
+        result = sums[i] + multiply(turned[i], [table[0, i, c] for c in range(WIDTH // 128)])
         for b in range(blocks):
             size = min(WIDTH, width - b * WIDTH)
             col = lax.broadcasted_iota(jnp.int32, (layers, size), 1) + b * WIDTH
@@ -410,40 +460,48 @@
             out_ref[i, :, b * WIDTH : b * WIDTH + size] = piece
 
 
-def synthesis(received, table, wave_pair, lat_slot, waves):
-    wav_count, slots, both, _ = received.shape
+def synthesis(late, table, sums, wave_pair, lat_slot, slots, waves):
+    held, wav_count, both, _ = late.shape
     rows = both // 2
-    total = wav_count * slots
+    total = wave_pair.shape[0]
     layers = 64
     width = 2 * NLAT + 16
-    blocks = (width + WIDTH - 1) // WIDTH
     together = 2
-    flat = received.reshape(total * both, 128)
+    flat = late.reshape(held * wav_count * both, 128)
     return pl.pallas_call(
-        functools.partial(synthesis_kernel, waves, rows, together),
+        functools.partial(synthesis_kernel, waves, rows, together, slots),
         grid=(rows // together,),
         out_shape=jax.ShapeDtypeStruct((rows, layers, width), jnp.bfloat16),
         in_specs=[
             pl.BlockSpec((1, total), lambda r: (0, 0)),
             pl.BlockSpec(memory_space=pltpu.SMEM),
-            pl.BlockSpec((total * both, 128), lambda r: (0, 0)),
-            pl.BlockSpec((together, WIDTH // 128, 1024, 128), lambda r: (r, 0, 0, 0)),
+            pl.BlockSpec(flat.shape, lambda r: (0, 0)),
+            pl.BlockSpec((1, together, *table.shape[2:]), lambda r: (1, r, 0, 0, 0)),
+            pl.BlockSpec((together, *sums.shape[1:]), lambda r: (r, 0, 0)),
         ],
         out_specs=pl.BlockSpec((together, layers, width), lambda r: (r, 0, 0)),
         scratch_shapes=[
-            pltpu.VMEM((total * PITCH, 128), jnp.float32),
+            pltpu.VMEM((held * wav_count * PITCH, 128), jnp.float32),
+            pltpu.VMEM((8, 128), jnp.float32),
         ]
-        + [pltpu.VMEM((8, blocks * layers, 128), jnp.bfloat16)] * together,
+        + [pltpu.VMEM((4, sums.shape[1], 128), jnp.bfloat16)] * together,
         compiler_params=pltpu.CompilerParams(
             dimension_semantics=("arbitrary",), vmem_limit_bytes=GRANT
         ),
         name="synthesis",
-    )(wave_pair.reshape(1, total), lat_slot, flat, table)
+    )(
+        pltpu.with_memory_space_constraint(wave_pair.reshape(1, total), pltpu.HBM),
+        pltpu.with_memory_space_constraint(lat_slot, pltpu.HBM),
+        flat,
+        table,
+        sums,
+    )
 
 
 def on_device(spectral, legendre, wave_pair, lat_slot):
-    received, table = exchange(spectral, legendre, wave_pair, lat_slot)
-    return synthesis(received, table, wave_pair, lat_slot, spectral.shape[1] - 1)
+    late, table, sums = exchange(spectral, legendre, wave_pair, lat_slot)
+    slots, fold, _ = spectral.shape
+    return synthesis(late, table, sums, wave_pair, lat_slot, slots, fold - 1)
 
 
 def solution(mesh):

time: 46.6 us -> 44.1 us (0.946)
  local copies, waits for them, and re-layouts: 1.35 us -> 0 us
  Pallas kernels: 45.1 us -> 44 us
    unnamed x4 -> x0, local copies, waits for them, and re-layouts: 1.35 us -> none
    pallas_call x1, Pallas kernels: 5.7 us -> 4.59 us  [synthesis(): pl.pallas_call(functools.partial(synthesis_kernel, waves, rows, together,...]
where the time goes in v5:
time: 44.1 us; the launch traced here: 44 us
  Pallas kernels  44 us (100%)
    pallas_call x1, Pallas kernels, exchange(): pl.pallas_call(functools.partial(exchange_kernel, fold - 1, slots, fold,...  39.4 us
    pallas_call x1, Pallas kernels, synthesis(): pl.pallas_call(functools.partial(synthesis_kernel, waves, rows, together,...  4.59 us

profile of v5, /device:TPU:1, one launch (start us, length us, event | category | flops | bytes accessed | tf_op | source)
XLA Modules:
  0.0 44.0 jit_solution(1249517940356726070)
XLA Ops:
  0.0 39.4 %exchange.1 = (bf16[4,32,16,128]{3,2,1,0:T(8,128)(2,1)S(1)}, bf16[2,8,2,512,128]{4,3,2,1,0:T(8,128)(2,1)S(1)}, f32[8,448,256]{2,1,0:T(8,128)S(1)}) custom-call(s32[224]{0:T(256)} %pair_hbm.1, s32[1,224]{1,0:T(1,128)} %bitcast.5, s32[256]{0:T(256)} %lat_ref.1, bf16[7,32,401]{2,1,0:T(8,128)(2,1)} %bitcast.4, bf16[7,401,128]{2,1,0:T(8,128)(2,1)} %spec_hbm.1), custom_call_target="tpu_custom_call" | custom-call | tf_op jit(solution)/shard_map/exchange/pallas_call | solution.py:397
  39.4 4.6 %synthesis.1 = bf16[8,64,1616]{2,1,0:T(8,128)(2,1)} custom-call(s32[1,224]{1,0:T(1,128)} %bitcast.6, s32[256]{0:T(256)} %lat_ref.1, bf16[2048,128]{1,0:T(8,128)(2,1)S(1)} %bitcast.3, bf16[2,8,2,512,128]{4,3,2,1,0:T(8,128)(2,1)S(1)} %get-tuple-element.9.table, f32[8,448,256]{2,1,0:T(8,128)S(1)} %get-tuple-element.10.sums), custom_call_target="tpu_custom_call" | custom-call | tf_op jit(solution)/shard_map/synthesis/pallas_call | solution.py:471

commit v6 on v5

--- a/solution.py
+++ b/solution.py
@@ -61,13 +61,12 @@
     lax.fori_loop(0, count, piece, 0, unroll=16)
 
 
-def turn_row(waves, rows, layers, blocks, count, pairs, flat, r, lon, turned):
+def turn_row(waves, rows, layers, blocks, count, pairs, flat, r, points, turned):
     target = lax.broadcasted_iota(jnp.int32, (128, 128), 0)
     source = lax.broadcasted_iota(jnp.int32, (128, 128), 1)
     part = (target >= layers).astype(jnp.int32)
     place = (source == 2 * (target - part * layers) + part).astype(jnp.bfloat16)
     shift = lax.broadcasted_iota(jnp.int32, (8, count), 0).astype(jnp.float32) * WIDTH
-    points = jnp.full((8, count), lon.astype(jnp.float32), jnp.float32)
     inverse = 1.0 / points
     for h in range(2):
         values = flat[pl.ds(h * rows + r, count, stride=PITCH), :].astype(jnp.bfloat16)
@@ -111,6 +110,8 @@
     late_ref,
     table,
     sums,
+    lanes,
+    lengths,
     pair_ref,
     pairs_ref,
     lat_ref,
@@ -120,7 +121,6 @@
     rhs,
     ready,
     column,
-    lanes,
     early,
     flat,
     turned,
@@ -348,8 +348,8 @@
     turned[...] = jnp.zeros_like(turned)
 
     def one_row(r, _):
-        lon = longitudes(lat_ref[w * rows + r])
-        turn_row(waves, rows, 64, sums.shape[1] // 64, EARLY * wav_count, lanes[:, :128], flat, r, lon, turned)
+        lengths[r] = jnp.full((8, 128), longitudes(lat_ref[w * rows + r]).astype(jnp.float32), jnp.float32)
+        turn_row(waves, rows, 64, sums.shape[1] // 64, EARLY * wav_count, lanes[:, :128], flat, r, lengths[r][:, : EARLY * wav_count], turned)
         sums[r] = multiply(turned, [table[0, r, c] for c in range(WIDTH // 128)])
         return 0
 
@@ -400,9 +400,11 @@
             jax.ShapeDtypeStruct((slots - EARLY, wav_count, 2 * rows, 128), jnp.bfloat16),
             jax.ShapeDtypeStruct((2, rows, WIDTH // 128, 512, 128), jnp.bfloat16),
             jax.ShapeDtypeStruct((rows, moved, WIDTH), jnp.float32),
+            jax.ShapeDtypeStruct((8, 256), jnp.float32),
+            jax.ShapeDtypeStruct((rows, 8, 128), jnp.float32),
         ],
         in_specs=[pl.BlockSpec(memory_space=pl.ANY)] * 5,
-        out_specs=[pl.BlockSpec(memory_space=pltpu.VMEM)] * 3,
+        out_specs=[pl.BlockSpec(memory_space=pltpu.VMEM)] * 5,
         scratch_shapes=[
             pltpu.SMEM(wave_pair.shape, jnp.int32),
             pltpu.VMEM((1, total), jnp.int32),
@@ -413,7 +415,6 @@
             pltpu.VMEM((slots, 512, 256), jnp.bfloat16),
             pltpu.VMEM((slots, wav_count, 2 * rows, 128), jnp.bfloat16),
             pltpu.VMEM((256, 128), jnp.float32),
-            pltpu.VMEM((8, 256), jnp.float32),
             pltpu.VMEM((EARLY, wav_count, 2 * rows, 128), jnp.bfloat16),
             pltpu.VMEM((EARLY * wav_count * PITCH, 128), jnp.float32),
             pltpu.VMEM((4, moved, 128), jnp.bfloat16),
@@ -430,78 +431,69 @@
     )(*(pltpu.with_memory_space_constraint(x, pltpu.HBM) for x in (wave_pair, wave_pair.reshape(1, total), lat_slot, turned, spectral)))
 
 
-def synthesis_kernel(waves, rows, together, slots, pair_ref, lat_ref, in_ref, table, sums, out_ref, flat, lanes, *turned):
+def synthesis_kernel(waves, together, in_ref, table, sums, lanes, lengths, out_ref, flat, *turned):
     step = pl.program_id(0)
     layers = out_ref.shape[1]
     width = out_ref.shape[2]
     blocks = (width + WIDTH - 1) // WIDTH
-    count = in_ref.shape[0] // (2 * rows)
+    count = flat.shape[0] // PITCH
+    both = in_ref.shape[0] // count
 
     @pl.when(step == 0)
     def _():
-        unpack(flat, in_ref, count, 2 * rows)
-        lanes[...] = lined_up(pair_ref[...].astype(jnp.float32), EARLY, slots, lax.axis_size("wav"), slots)
-        for buffer in turned:
-            buffer[...] = jnp.zeros_like(buffer)
-
-    lengths = []
+        unpack(flat, in_ref, count, both)
+        if count < 128:
+            for buffer in turned:
+                buffer[...] = jnp.zeros_like(buffer)
+
     for i in range(together):
         r = step * together + i
-        lengths.append(longitudes(lat_ref[lax.axis_index("wav") * rows + r]))
-        turn_row(waves, rows, layers, blocks, count, lanes[...], flat, r, lengths[i], turned[i])
+        turn_row(waves, both // 2, layers, blocks, count, lanes[:, 128:], flat, r, lengths[i][:, :count], turned[i])
 
     for i in range(together):
         result = sums[i] + multiply(turned[i], [table[0, i, c] for c in range(WIDTH // 128)])
+        length = jnp.concatenate([lengths[i][:1]] * (WIDTH // 128), axis=1)
         for b in range(blocks):
             size = min(WIDTH, width - b * WIDTH)
-            col = lax.broadcasted_iota(jnp.int32, (layers, size), 1) + b * WIDTH
+            col = (lax.broadcasted_iota(jnp.int32, (layers, size), 1) + b * WIDTH).astype(jnp.float32)
             piece = result[b * layers : (b + 1) * layers, :size]
-            piece = jnp.where(col < lengths[i], piece, 0.0).astype(jnp.bfloat16)
+            piece = jnp.where(col < length[:, :size], piece, 0.0).astype(jnp.bfloat16)
             out_ref[i, :, b * WIDTH : b * WIDTH + size] = piece
 
 
-def synthesis(late, table, sums, wave_pair, lat_slot, slots, waves):
+def synthesis(late, table, sums, lanes, lengths, waves):
     held, wav_count, both, _ = late.shape
     rows = both // 2
-    total = wave_pair.shape[0]
     layers = 64
     width = 2 * NLAT + 16
     together = 2
     flat = late.reshape(held * wav_count * both, 128)
     return pl.pallas_call(
-        functools.partial(synthesis_kernel, waves, rows, together, slots),
+        functools.partial(synthesis_kernel, waves, together),
         grid=(rows // together,),
         out_shape=jax.ShapeDtypeStruct((rows, layers, width), jnp.bfloat16),
         in_specs=[
-            pl.BlockSpec((1, total), lambda r: (0, 0)),
-            pl.BlockSpec(memory_space=pltpu.SMEM),
             pl.BlockSpec(flat.shape, lambda r: (0, 0)),
             pl.BlockSpec((1, together, *table.shape[2:]), lambda r: (1, r, 0, 0, 0)),
             pl.BlockSpec((together, *sums.shape[1:]), lambda r: (r, 0, 0)),
+            pl.BlockSpec(lanes.shape, lambda r: (0, 0)),
+            pl.BlockSpec((together, *lengths.shape[1:]), lambda r: (r, 0, 0)),
         ],
         out_specs=pl.BlockSpec((together, layers, width), lambda r: (r, 0, 0)),
         scratch_shapes=[
             pltpu.VMEM((held * wav_count * PITCH, 128), jnp.float32),
-            pltpu.VMEM((8, 128), jnp.float32),
         ]
         + [pltpu.VMEM((4, sums.shape[1], 128), jnp.bfloat16)] * together,
         compiler_params=pltpu.CompilerParams(
             dimension_semantics=("arbitrary",), vmem_limit_bytes=GRANT
         ),
         name="synthesis",
-    )(
-        pltpu.with_memory_space_constraint(wave_pair.reshape(1, total), pltpu.HBM),
-        pltpu.with_memory_space_constraint(lat_slot, pltpu.HBM),
-        flat,
-        table,
-        sums,
-    )
+    )(flat, table, sums, lanes, lengths)
 
 
 def on_device(spectral, legendre, wave_pair, lat_slot):
-    late, table, sums = exchange(spectral, legendre, wave_pair, lat_slot)
-    slots, fold, _ = spectral.shape
-    return synthesis(late, table, sums, wave_pair, lat_slot, slots, fold - 1)
+    late, table, sums, lanes, lengths = exchange(spectral, legendre, wave_pair, lat_slot)
+    return synthesis(late, table, sums, lanes, lengths, spectral.shape[1] - 1)
 
 
 def solution(mesh):

time: 44.1 us -> 43 us (0.975)
  Pallas kernels: 44 us -> 42.9 us
    pallas_call x1, Pallas kernels: 4.59 us -> 3.48 us  [synthesis(): pl.pallas_call(functools.partial(synthesis_kernel, waves, together), grid...]
where the time goes in v6:
time: 43 us; the launch traced here: 42.9 us
  Pallas kernels  42.9 us (100%)
    pallas_call x1, Pallas kernels, exchange(): pl.pallas_call(functools.partial(exchange_kernel, fold - 1, slots, fold,...  39.4 us
    pallas_call x1, Pallas kernels, synthesis(): pl.pallas_call(functools.partial(synthesis_kernel, waves, together), grid...  3.48 us

profile of v6, /device:TPU:1, one launch (start us, length us, event | category | flops | bytes accessed | tf_op | source)
XLA Modules:
  0.0 42.9 jit_solution(700207376798950025)
XLA Ops:
  0.0 39.4 %exchange.1 = (bf16[4,32,16,128]{3,2,1,0:T(8,128)(2,1)S(1)}, bf16[2,8,2,512,128]{4,3,2,1,0:T(8,128)(2,1)S(1)}, f32[8,448,256]{2,1,0:T(8,128)S(1)}, f32[8,256]{1,0:T(8,128)S(1)}, f32[8,8,128]{2,1,0:T(8,128)S(1)}) custom-call(s32[224]{0:T(256)} %pair_hbm.1, s32[1,224]{1,0:T(1,128)} %bitcast.5, s32[256]{0:T(256)} %lat_hbm.1, bf16[7,32,401]{2,1,0:T(8,128)(2,1)} %bitcast.4, ...), custom_call_target="tpu_custom_call" | custom-call | tf_op jit(solution)/shard_map/exchange/pallas_call | solution.py:397
  39.4 3.5 %synthesis.1 = bf16[8,64,1616]{2,1,0:T(8,128)(2,1)} custom-call(bf16[2048,128]{1,0:T(8,128)(2,1)S(1)} %bitcast.3, bf16[2,8,2,512,128]{4,3,2,1,0:T(8,128)(2,1)S(1)} %get-tuple-element.11.table, f32[8,448,256]{2,1,0:T(8,128)S(1)} %get-tuple-element.12.sums, f32[8,256]{1,0:T(8,128)S(1)} %get-tuple-element.13.lanes, f32[8,8,128]{2,1,0:T(8,128)S(1)} %get-tuple-element.14.lengths), custom_call_target="tpu_custom_call" | custom-call | tf_op jit(solution)/shard_map/synthesis/pallas_call | solution.py:471

commit v7 on v6

--- a/solution.py
+++ b/solution.py
@@ -466,7 +466,7 @@
     rows = both // 2
     layers = 64
     width = 2 * NLAT + 16
-    together = 2
+    together = 4
     flat = late.reshape(held * wav_count * both, 128)
     return pl.pallas_call(
         functools.partial(synthesis_kernel, waves, together),

time: 43 us -> 42.5 us (0.988)
  Pallas kernels: 42.9 us -> 42.4 us
    pallas_call x1, Pallas kernels: 3.48 us -> 2.97 us  [synthesis(): pl.pallas_call(functools.partial(synthesis_kernel, waves, together), grid...]
where the time goes in v7:
time: 42.5 us; the launch traced here: 42.4 us
  Pallas kernels  42.4 us (100%)
    pallas_call x1, Pallas kernels, exchange(): pl.pallas_call(functools.partial(exchange_kernel, fold - 1, slots, fold,...  39.4 us
    pallas_call x1, Pallas kernels, synthesis(): pl.pallas_call(functools.partial(synthesis_kernel, waves, together), grid...  2.97 us

profile of v7, /device:TPU:1, one launch (start us, length us, event | category | flops | bytes accessed | tf_op | source)
XLA Modules:
  0.0 42.4 jit_solution(12887707338091880046)
XLA Ops:
  0.0 39.4 %exchange.1 = (bf16[4,32,16,128]{3,2,1,0:T(8,128)(2,1)S(1)}, bf16[2,8,2,512,128]{4,3,2,1,0:T(8,128)(2,1)S(1)}, f32[8,448,256]{2,1,0:T(8,128)S(1)}, f32[8,256]{1,0:T(8,128)S(1)}, f32[8,8,128]{2,1,0:T(8,128)S(1)}) custom-call(s32[224]{0:T(256)} %pair_hbm.1, s32[1,224]{1,0:T(1,128)} %bitcast.5, s32[256]{0:T(256)} %lat_hbm.1, bf16[7,32,401]{2,1,0:T(8,128)(2,1)} %bitcast.4, ...), custom_call_target="tpu_custom_call" | custom-call | tf_op jit(solution)/shard_map/exchange/pallas_call | solution.py:397
  39.4 3.0 %synthesis.1 = bf16[8,64,1616]{2,1,0:T(8,128)(2,1)} custom-call(bf16[2048,128]{1,0:T(8,128)(2,1)S(1)} %bitcast.3, bf16[2,8,2,512,128]{4,3,2,1,0:T(8,128)(2,1)S(1)} %get-tuple-element.11.table, f32[8,448,256]{2,1,0:T(8,128)S(1)} %get-tuple-element.12.sums, f32[8,256]{1,0:T(8,128)S(1)} %get-tuple-element.13.lanes, f32[8,8,128]{2,1,0:T(8,128)S(1)} %get-tuple-element.14.lengths), custom_call_target="tpu_custom_call" | custom-call | tf_op jit(solution)/shard_map/synthesis/pallas_call | solution.py:471

commit v8 on v7

--- a/solution.py
+++ b/solution.py
@@ -353,7 +353,7 @@
         sums[r] = multiply(turned, [table[0, r, c] for c in range(WIDTH // 128)])
         return 0
 
-    lax.fori_loop(0, rows, one_row, 0)
+    lax.fori_loop(0, rows, one_row, 0, unroll=2)
 
     for side in (0, 1):
         for d in range(half):

time: 42.5 us -> 42.2 us (level)
  no operation moved by 1% of the time
where the time goes in v8:
time: 42.2 us; the launch traced here: 42.1 us
  Pallas kernels  42.1 us (100%)
    pallas_call x1, Pallas kernels, exchange(): pl.pallas_call(functools.partial(exchange_kernel, fold - 1, slots, fold,...  39.2 us
    pallas_call x1, Pallas kernels, synthesis(): pl.pallas_call(functools.partial(synthesis_kernel, waves, together), grid...  2.96 us

profile of v8, /device:TPU:1, one launch (start us, length us, event | category | flops | bytes accessed | tf_op | source)
XLA Modules:
  0.0 42.1 jit_solution(4517785158733364194)
XLA Ops:
  0.0 39.2 %exchange.1 = (bf16[4,32,16,128]{3,2,1,0:T(8,128)(2,1)S(1)}, bf16[2,8,2,512,128]{4,3,2,1,0:T(8,128)(2,1)S(1)}, f32[8,448,256]{2,1,0:T(8,128)S(1)}, f32[8,256]{1,0:T(8,128)S(1)}, f32[8,8,128]{2,1,0:T(8,128)S(1)}) custom-call(s32[224]{0:T(256)} %pair_hbm.1, s32[1,224]{1,0:T(1,128)} %bitcast.5, s32[256]{0:T(256)} %lat_hbm.1, bf16[7,32,401]{2,1,0:T(8,128)(2,1)} %bitcast.4, ...), custom_call_target="tpu_custom_call" | custom-call | tf_op jit(solution)/shard_map/exchange/pallas_call | solution.py:397
  39.2 3.0 %synthesis.1 = bf16[8,64,1616]{2,1,0:T(8,128)(2,1)} custom-call(bf16[2048,128]{1,0:T(8,128)(2,1)S(1)} %bitcast.3, bf16[2,8,2,512,128]{4,3,2,1,0:T(8,128)(2,1)S(1)} %get-tuple-element.11.table, f32[8,448,256]{2,1,0:T(8,128)S(1)} %get-tuple-element.12.sums, f32[8,256]{1,0:T(8,128)S(1)} %get-tuple-element.13.lanes, f32[8,8,128]{2,1,0:T(8,128)S(1)} %get-tuple-element.14.lengths), custom_call_target="tpu_custom_call" | custom-call | tf_op jit(solution)/shard_map/synthesis/pallas_call | solution.py:471
